TPU v7x, 256 devices: a whole 4x4x8 slice. The times are simulated.
256 devices in a mesh: dp: 16 (over z, core), ctx: 16 (over x, y).
Axes of the slice: x: 4, y: 4, z: 8, core: 2. Of those that a mesh axis runs over, the one named last changes fastest.
Arguments:
- hidden: bfloat16 [16, 2048, 5120], P('dp', 'ctx'), may hold values from -6 to 6
- queries: bfloat16 [16, 2048, 4096], P('dp', 'ctx'), may hold values from -6 to 6
- key_states: bfloat16 [16, 2048, 512], P('dp', 'ctx'), may hold values from -6 to 6
- out_grad: bfloat16 [16, 2048, 4096], P('dp', 'ctx'), may hold values from -6 to 6
- w_value: bfloat16 [5120, 512], replicated, may hold values from -0.078125 to 0.078125
- q_gain: float32 [128], replicated, may hold values from 0.1 to 1.9
- k_gain: float32 [128], replicated, may hold values from 0.1 to 1.9
- dest_rows: int32 [16, 2048], P('dp', 'ctx'), may hold values from 0 to 2047, as said below
- doc_ids: int32 [16, 2048], P('dp', 'ctx'), may hold values from 0 to 3, never falling along the last dimension, each value on 1 to 1024 neighbouring positions
Outputs:
- hidden_grad: bfloat16 [16, 2048, 5120], P('dp', 'ctx')
- query_grad: bfloat16 [16, 2048, 4096], P('dp', 'ctx')
- key_grad: bfloat16 [16, 2048, 512], P('dp', 'ctx')
- weight_grad: float32 [5120, 512], P(('dp', 'ctx'))
Inputs may be any that keep to these rules, and one draw needn't show every extreme that they name: `dest_rows`: within each data group the entries are a permutation of the slab's rows; the 128 entries of one block of arrival rows name exactly 16 or no rows of each block of 128 slab rows. `doc_ids`: ids never fall along a slab.
All inputs are finite; a program needn't handle non-finite values.
Results may differ from a plain program's by a relative error of at most 0.017.
Values may be sent and summed in bfloat16 or wider, within the bound.
A program may use at most 128 MiB of HBM per device.

v0:
```python
import functools
import math

import jax
import jax.numpy as jnp
import numpy as np
from jax import lax
from jax.experimental import pallas as pl
from jax.experimental.pallas import tpu as pltpu
from jax.sharding import PartitionSpec as P

epsilon = 1e-06
rope_base = 1000000.0
BF16, F32, I32 = jnp.bfloat16, jnp.float32, jnp.int32
ANY = pl.BlockSpec(memory_space=pl.ANY)
VMEM = pl.BlockSpec(memory_space=pltpu.VMEM)
TILE = 256
NT = (((1,), (1,)), ((), ()))
TN = (((0,), (0,)), ((), ()))


def dot(a, b, dims=(((1,), (0,)), ((), ()))):
    return lax.dot_general(a, b, dims, preferred_element_type=F32)


def send(src, dst, ssem, rsem, dp, ctx):
    return pltpu.make_async_remote_copy(
        src_ref=src,
        dst_ref=dst,
        send_sem=ssem,
        recv_sem=rsem,
        device_id=(dp, ctx),
        device_id_type=pl.DeviceIdType.MESH,
    )


def signal(sem, dp, ctx):
    pl.semaphore_signal(
        sem, inc=1, device_id=(dp, ctx), device_id_type=pl.DeviceIdType.MESH
    )


def window(dp, share):
    return pl.multiple_of((dp * share) // 128 * 128, 128)


def arrive_kernel(
    sizes, q, g, k, h, w, index, q_o, g_o, k_o, v_o, index_o, hf_o,
    h_v, w_v, v_v, ssem, rsem, hssem, hrsem, lsem,
):
    n_dp, n_ctx, rows, width, head, per_kv, share, win = sizes
    dp, me = lax.axis_index("dp"), lax.axis_index("ctx")

    load_h = pltpu.make_async_copy(h, h_v, lsem.at[6])
    load_w = pltpu.make_async_copy(w, w_v, lsem.at[7])
    load_h.start()
    load_w.start()

    barrier = pltpu.get_barrier_semaphore()

    @pl.loop(1, n_ctx)
    def _(d):
        signal(barrier, dp, lax.rem(me + d, n_ctx))

    @pl.loop(1, n_dp)
    def _(d):
        signal(barrier, lax.rem(dp + d, n_dp), me)

    pl.semaphore_wait(barrier, n_ctx - 1 + n_dp - 1)

    def cols(s, size):
        return pl.ds(pl.multiple_of(s * size, size), size)

    def block(c):
        return pl.ds(pl.multiple_of(c * rows, rows), rows)

    def pieces(to, frm):
        return (
            (index, index_o.at[frm]),
            (k.at[:, cols(to // per_kv, head)], k_o.at[block(frm), :]),
            (q.at[:, cols(to, width)], q_o.at[block(frm), :]),
            (g.at[:, cols(to, width)], g_o.at[block(frm), :]),
            (v_v.at[:, cols(to // per_kv, head)], v_o.at[block(frm), :]),
        )

    def ctx_copy(kind, d, to, frm):
        src, dst = pieces(to, frm)[kind]
        return send(src, dst, ssem.at[kind, d], rsem.at[kind, d], dp, to)

    def hf_copy(d, to, frm):
        return send(
            h_v.at[:, pl.ds(window(to, share), win)],
            hf_o.at[frm],
            hssem.at[d],
            hrsem.at[d],
            to,
            me,
        )

    for kind in range(4):

        @pl.loop(1, n_ctx)
        def _(d, kind=kind):
            ctx_copy(kind, d, lax.rem(me + d, n_ctx), me).start()

    local = [
        pltpu.make_async_copy(src, dst, lsem.at[i])
        for i, (src, dst) in enumerate(pieces(me, me)[:4])
    ]
    for copy in local:
        copy.start()
    load_h.wait()

    @pl.loop(1, n_dp)
    def _(d):
        hf_copy(d, lax.rem(dp + d, n_dp), dp).start()

    own_hf = pltpu.make_async_copy(
        h_v.at[:, pl.ds(window(dp, share), win)], hf_o.at[dp], lsem.at[5]
    )
    own_hf.start()
    load_w.wait()
    v_v[...] = dot(h_v[...], w_v[...]).astype(BF16)

    @pl.loop(1, n_ctx)
    def _(d):
        ctx_copy(4, d, lax.rem(me + d, n_ctx), me).start()

    src, dst = pieces(me, me)[4]
    own_v = pltpu.make_async_copy(src, dst, lsem.at[4])
    own_v.start()
    for copy in local:
        copy.wait()
    own_hf.wait()
    own_v.wait()
    for kind in range(5):

        @pl.loop(1, n_ctx)
        def _(d, kind=kind):
            ctx_copy(kind, d, lax.rem(me + d, n_ctx), me).wait_send()
            frm = lax.rem(me + n_ctx - d, n_ctx)
            ctx_copy(kind, d, me, frm).wait_recv()

    @pl.loop(1, n_dp)
    def _(d):
        hf_copy(d, lax.rem(dp + d, n_dp), dp).wait_send()
        frm = lax.rem(dp + n_dp - d, n_dp)
        hf_copy(d, dp, frm).wait_recv()


def attend_kernel(
    sizes, q_ref, g_ref, k_ref, v_ref, dest_ref, ids_ref, qg_ref, kg_ref, fr_ref, clo_ref, slo_ref,
    gq_ref, gk_ref, gv_ref, ga_ref,
    qs, gs, kn, vs, cs, sn, es, ds_, gk_acc, gv_acc,
):
    slab, heads, head, n_docs = sizes
    tiles = slab // TILE
    factor = head ** (-0.5)
    half = head // 2

    ids = ids_ref[...]
    counts = [jnp.sum((ids < d).astype(F32)) for d in range(1, n_docs)]
    bounds = [c.astype(I32) for c in counts]

    def start_of(row):
        start = jnp.zeros_like(row)
        for b in bounds:
            start = jnp.where(row >= b, b, start)
        return start

    q_gain = qg_ref[...]
    k_gain = kg_ref[...]
    lane = lax.broadcasted_iota(I32, (1, head), 1)
    sign = jnp.where(lane < half, -1.0, 1.0).astype(F32)

    def normrope(u, gain, c, s):
        inv = lax.rsqrt(jnp.mean(u * u, axis=-1, keepdims=True) + epsilon)
        y = u * inv * gain
        return y * c + pltpu.roll(y, half, 1) * s

    def normrope_back(u, gz, gain, c, s):
        inv = lax.rsqrt(jnp.mean(u * u, axis=-1, keepdims=True) + epsilon)
        hat = u * inv
        gn = (gz * c - pltpu.roll(gz, half, 1) * s) * gain
        return inv * (gn - hat * jnp.mean(gn * hat, axis=-1, keepdims=True))

    @pl.loop(0, tiles)
    def _(i):
        r0 = pl.multiple_of(i * TILE, TILE)
        at = pl.ds(r0, TILE)
        row = lax.broadcasted_iota(I32, (TILE, 1), 0) + r0
        base = [jnp.zeros((), I32)] + bounds
        c0 = s0 = None
        for d, b in enumerate(base):
            angle = (r0 - b).astype(F32) * fr_ref[...]
            c_d, s_d = jnp.cos(angle)[:1], jnp.sin(angle)[:1]
            if d == 0:
                c0 = jnp.broadcast_to(c_d, (TILE, head))
                s0 = jnp.broadcast_to(s_d, (TILE, head))
            else:
                c0 = jnp.where(row >= b, c_d, c0)
                s0 = jnp.where(row >= b, s_d, s0)
        clo, slo = clo_ref[...], slo_ref[...]
        c = clo * c0 - slo * s0
        s = (slo * c0 + clo * s0) * sign
        cs[at, :] = c
        sn[at, :] = s
        for hd in range(heads):
            lanes = slice(hd * head, (hd + 1) * head)
            to = slice(hd * TILE, (hd + 1) * TILE)
            u = q_ref[at, lanes].astype(F32)
            qs[i, to, :] = normrope(u, q_gain, c, s).astype(BF16)
            gs[i, to, :] = g_ref[at, lanes]
        kn[at, :] = normrope(k_ref[at, :].astype(F32), k_gain, c, s).astype(BF16)
        gk_acc[at, :] = jnp.zeros((TILE, head), F32)
        gv_acc[at, :] = jnp.zeros((TILE, head), F32)

    def placing(i):
        row = lax.broadcasted_iota(I32, (TILE, 1), 0) + i * TILE
        return jnp.where(row == dest_ref[...], 1.0, 0.0).astype(BF16)

    @pl.loop(0, tiles)
    def _(i):
        r0 = pl.multiple_of(i * TILE, TILE)
        vs[pl.ds(r0, TILE), :] = dot(placing(i), v_ref[...]).astype(BF16)

    scale = factor * math.log2(math.e)

    @pl.loop(0, tiles)
    def _(i):
        r0 = pl.multiple_of(i * TILE, TILE)
        row = lax.broadcasted_iota(I32, (1, TILE), 1) + r0
        start = start_of(row)
        first = jnp.zeros((), I32)
        for b in bounds:
            first = jnp.where(r0 >= b, b, first)
        low = first // TILE
        qi, gi = qs[i], gs[i]

        def forward(j, carry):
            total, num = carry
            k0 = pl.multiple_of(j * TILE, TILE)
            at = pl.ds(k0, TILE)
            key = lax.broadcasted_iota(I32, (TILE, 1), 0) + k0
            allowed = (key >= start) & (key <= row)
            logits = dot(kn[at, :], qi, NT) * scale
            pg = dot(vs[at, :], gi, NT)
            es_parts = []
            for hd in range(heads):
                lanes = slice(hd * TILE, (hd + 1) * TILE)
                es_parts.append(jnp.where(allowed, jnp.exp2(logits[:, lanes]), 0.0))
            e = jnp.concatenate(es_parts, axis=1)
            es[j] = e
            ds_[j] = pg
            total = total + jnp.sum(e, axis=0, keepdims=True)
            num = num + jnp.sum(e * pg, axis=0, keepdims=True)
            return total, num

        zero = jnp.zeros((1, heads * TILE), F32)
        total, num = lax.fori_loop(low, i + 1, forward, (zero, zero))
        inv = 1.0 / total
        delta = num * inv

        def backward(j, acc):
            at = pl.ds(pl.multiple_of(j * TILE, TILE), TILE)
            p = es[j] * inv
            dsj = (p * (ds_[j] - delta)).astype(BF16)
            gk_acc[at, :] += dot(dsj, qi)
            gv_acc[at, :] += dot(p.astype(BF16), gi)
            return acc + dot(dsj, kn[at, :], TN)

        acc = lax.fori_loop(low, i + 1, backward, jnp.zeros((heads * TILE, head), F32))
        at = pl.ds(r0, TILE)
        for hd in range(heads):
            lanes = slice(hd * head, (hd + 1) * head)
            gz = acc[hd * TILE : (hd + 1) * TILE] * factor
            u = q_ref[at, lanes].astype(F32)
            gq_ref[at, lanes] = normrope_back(u, gz, q_gain, cs[at, :], sn[at, :]).astype(BF16)

    @pl.loop(0, tiles)
    def _(i):
        at = pl.ds(pl.multiple_of(i * TILE, TILE), TILE)
        gz = gk_acc[at, :] * factor
        u = k_ref[at, :].astype(F32)
        gk_ref[at, :] = normrope_back(u, gz, k_gain, cs[at, :], sn[at, :]).astype(BF16)
        gv_ref[at, :] = gv_acc[at, :].astype(BF16)
        gv_acc[at, :] = jnp.zeros((TILE, head), F32)

    @pl.loop(0, tiles)
    def _(i):
        at = pl.ds(pl.multiple_of(i * TILE, TILE), TILE)
        gv_acc[...] += dot(placing(i), gv_ref[at, :], TN)

    ga_ref[...] = gv_acc[...].astype(BF16)


def return_kernel(
    sizes, gq, gk, gv, ga, w, hf, gq_o, gk_o, h_o, w_o,
    kr, vr, ar, vg, ag, w_v, hf_v, dw, dws, dwr,
    ssem, rsem, lsem, ag_s, ag_r, ws, wr,
):
    n_dp, n_ctx, rows, width, head, per_kv, share, win = sizes
    n_z = n_dp // 2
    dp, me = lax.axis_index("dp"), lax.axis_index("ctx")
    z, core = dp // 2, dp % 2
    after = lax.rem(z + 1, n_z) * 2 + core
    before = lax.rem(z + n_z - 1, n_z) * 2 + core
    twin = z * 2 + 1 - core
    ahead = n_z // 2
    behind = n_z - 1 - ahead
    kv = n_ctx // per_kv

    load_w = pltpu.make_async_copy(w, w_v, lsem.at[4])
    load_hf = pltpu.make_async_copy(hf, hf_v, lsem.at[5])
    load_w.start()
    load_hf.start()

    barrier = pltpu.get_barrier_semaphore()

    @pl.loop(1, n_ctx)
    def _(d):
        signal(barrier, dp, lax.rem(me + d, n_ctx))

    around = [after, before, twin] if n_z > 2 else ([after, twin] if n_z > 1 else [twin])
    for other in around:
        signal(barrier, other, me)
    pl.semaphore_wait(barrier, n_ctx - 1 + len(around))

    def block(c):
        return pl.ds(pl.multiple_of(c * rows, rows), rows)

    def pieces(to, frm):
        place = pl.ds(pl.multiple_of(frm * width, width), width)
        return (
            (ga.at[block(to), :], ar.at[frm]),
            (gv.at[block(to), :], vr.at[frm]),
            (gk.at[block(to), :], kr.at[frm]),
            (gq.at[block(to), :], gq_o.at[:, place]),
        )

    def ctx_copy(kind, d, to, frm):
        src, dst = pieces(to, frm)[kind]
        return send(src, dst, ssem.at[kind, d], rsem.at[kind, d], dp, to)

    local = []
    for kind in range(4):

        @pl.loop(1, n_ctx)
        def _(d, kind=kind):
            ctx_copy(kind, d, lax.rem(me + d, n_ctx), me).start()

        src, dst = pieces(me, me)[kind]
        local.append(pltpu.make_async_copy(src, dst, lsem.at[kind]))
        local[-1].start()

    def arrived(kind):
        local[kind].wait()

        @pl.loop(1, n_ctx)
        def _(d):
            ctx_copy(kind, d, me, lax.rem(me + n_ctx - d, n_ctx)).wait_recv()

    def sums(ref, head_index):
        total = ref[head_index * per_kv].astype(F32)
        for s in range(1, per_kv):
            total = total + ref[head_index * per_kv + s].astype(F32)
        return total.astype(BF16)

    arrived(0)
    for hd in range(kv):
        ag[dp, :, hd * head : (hd + 1) * head] = sums(ar, hd)
    chunk = kv * head // 2

    def part(slot, ch):
        return ag.at[slot, :, pl.ds(ch * chunk, chunk)]

    def ring(slot, ch, way, to):
        return send(part(slot, ch), part(slot, ch), ag_s.at[slot, way, ch], ag_r.at[slot, ch], to, me)

    sent = []

    def go(slot, ch, way, to):
        copy = ring(slot, ch, way, to)
        copy.start()
        sent.append(copy)

    for ch in range(2):
        if ahead:
            go(dp, ch, 0, after)
        if behind:
            go(dp, ch, 1, before)
    for ch in range(2):
        go(dp, ch, 2, twin)

    load_w.wait()
    arrived(1)
    for hd in range(kv):
        vg[:, hd * head : (hd + 1) * head] = sums(vr, hd)

    model = h_o.shape[1]
    steps = max(ahead, 1)
    piece = model // steps
    sub = 256 if piece % 256 == 0 else piece
    for t in range(1, steps + 1):

        @pl.loop(0, piece // sub)
        def _(n, t=t):
            at = pl.ds(pl.multiple_of((t - 1) * piece + n * sub, sub), sub)
            h_o[:, at] = dot(vg[...], w_v[at, :], NT).astype(BF16)

        for ch in range(2):
            if t <= ahead:
                slot = lax.rem(z + n_z - t, n_z) * 2 + core
                ring(slot, ch, 0, after).wait_recv()
                if t < ahead:
                    go(slot, ch, 0, after)
                go(slot, ch, 2, twin)
            if t <= behind:
                slot = lax.rem(z + t, n_z) * 2 + core
                ring(slot, ch, 1, before).wait_recv()
                if t < behind:
                    go(slot, ch, 1, before)
                go(slot, ch, 2, twin)

    arrived(2)
    for hd in range(kv):
        gk_o[:, hd * head : (hd + 1) * head] = sums(kr, hd)
    for t in range(n_z):
        slot = lax.rem(z + t, n_z) * 2 + 1 - core
        for ch in range(2):
            ring(slot, ch, 2, twin).wait_recv()

    load_hf.wait()
    group = 4

    for n in range(n_dp // group):
        at = slice(n * group, (n + 1) * group)
        a = hf_v[at].reshape(group * rows, win)
        b = ag[at].reshape(group * rows, kv * head)
        part_sum = dot(a, b, TN)
        if n == 0:
            dw[...] = part_sum
        else:
            dw[...] += part_sum
    off = pl.multiple_of(dp * share - (dp * share) // 128 * 128, 64)
    out_rows = share // n_ctx
    pad = dws.shape[1]
    for c in range(n_ctx):
        dws[c, :out_rows, :] = dw[pl.ds(off, share), :][c * out_rows : (c + 1) * out_rows].astype(BF16)
        if pad > out_rows:
            dws[c, out_rows:, :] = jnp.zeros((pad - out_rows, kv * head), BF16)

    def w_copy(d, to, frm):
        return send(dws.at[to], dwr.at[frm], ws.at[d], wr.at[d], dp, to)

    @pl.loop(1, n_ctx)
    def _(d):
        w_copy(d, lax.rem(me + d, n_ctx), me).start()

    dwr[me] = dws[me]

    @pl.loop(1, n_ctx)
    def _(d):
        w_copy(d, me, lax.rem(me + n_ctx - d, n_ctx)).wait_recv()

    total = dwr[0].astype(F32)
    for c in range(1, n_ctx):
        total = total + dwr[c].astype(F32)
    w_o[...] = total[:out_rows] * (1.0 / (n_dp * n_ctx))

    arrived(3)
    for copy in sent:
        copy.wait_send()
    for kind in range(4):

        @pl.loop(1, n_ctx)
        def _(d, kind=kind):
            ctx_copy(kind, d, lax.rem(me + d, n_ctx), me).wait_send()

    @pl.loop(1, n_ctx)
    def _(d):
        w_copy(d, lax.rem(me + d, n_ctx), me).wait_send()


def on_device(hidden, queries, key_states, out_grad, w_value, q_gain, k_gain, dest_rows, doc_ids):
    n_dp, n_ctx = lax.axis_size("dp"), lax.axis_size("ctx")
    rows, model = hidden.shape[1:]
    head = q_gain.shape[0]
    kv_width = key_states.shape[2]
    kv = kv_width // head
    width = queries.shape[2] // n_ctx
    heads = width // head
    per_kv = n_ctx // kv
    slab = rows * n_ctx
    share = model // n_dp
    win = (share + 127) // 128 * 128
    sizes = (n_dp, n_ctx, rows, width, head, per_kv, share, win)
    sds = jax.ShapeDtypeStruct
    dma = pltpu.SemaphoreType.DMA

    index = jnp.concatenate([dest_rows, doc_ids], axis=0)
    q_in, g_in, k_in, v_in, index_in, hf = pl.pallas_call(
        functools.partial(arrive_kernel, sizes),
        out_shape=(
            sds((slab, width), BF16),
            sds((slab, width), BF16),
            sds((slab, head), BF16),
            sds((slab, head), BF16),
            sds((n_ctx, 2, rows), I32),
            sds((n_dp, rows, win), BF16),
        ),
        in_specs=[ANY] * 6,
        out_specs=(ANY,) * 6,
        scratch_shapes=[
            pltpu.VMEM((rows, model), BF16),
            pltpu.VMEM((model, kv_width), BF16),
            pltpu.VMEM((rows, kv_width), BF16),
            dma((5, n_ctx)),
            dma((5, n_ctx)),
            dma((n_dp,)),
            dma((n_dp,)),
            dma((8,)),
        ],
        compiler_params=pltpu.CompilerParams(
            collective_id=0, has_side_effects=True, vmem_limit_bytes=32 << 20
        ),
        name="arrive",
    )(queries[0], out_grad[0], key_states[0], hidden[0], w_value, index)

    dest_all = index_in[:, 0].reshape(1, slab)
    ids_all = index_in[:, 1]
    half = head // 2
    frequency = rope_base ** (-(np.arange(half, dtype=np.float64) * 2.0 / head))
    frequency = np.concatenate([frequency, frequency])[None]
    low = np.arange(TILE, dtype=np.float64)[:, None] * frequency
    consts = [
        jnp.asarray(np.broadcast_to(frequency, (8, head)), F32),
        jnp.asarray(np.cos(low), F32),
        jnp.asarray(np.sin(low), F32),
    ]
    tiles = slab // TILE
    gq, gk, gv, ga = pl.pallas_call(
        functools.partial(attend_kernel, (slab, heads, head, 4)),
        out_shape=(
            sds((slab, width), BF16),
            sds((slab, head), BF16),
            sds((slab, head), BF16),
            sds((slab, head), BF16),
        ),
        in_specs=[VMEM] * 11,
        out_specs=(VMEM,) * 4,
        scratch_shapes=[
            pltpu.VMEM((tiles, heads * TILE, head), BF16),
            pltpu.VMEM((tiles, heads * TILE, head), BF16),
            pltpu.VMEM((slab, head), BF16),
            pltpu.VMEM((slab, head), BF16),
            pltpu.VMEM((slab, head), F32),
            pltpu.VMEM((slab, head), F32),
            pltpu.VMEM((tiles, TILE, heads * TILE), F32),
            pltpu.VMEM((tiles, TILE, heads * TILE), F32),
            pltpu.VMEM((slab, head), F32),
            pltpu.VMEM((slab, head), F32),
        ],
        compiler_params=pltpu.CompilerParams(vmem_limit_bytes=48 << 20),
        name="attend",
    )(q_in, g_in, k_in, v_in, dest_all, ids_all, q_gain[None], k_gain[None], *consts)

    out_rows = share // n_ctx
    pad = (out_rows + 15) // 16 * 16
    query_grad, key_grad, hidden_grad, weight_grad = pl.pallas_call(
        functools.partial(return_kernel, sizes),
        out_shape=(
            sds((rows, n_ctx * width), BF16),
            sds((rows, kv_width), BF16),
            sds((rows, model), BF16),
            sds((out_rows, kv_width), F32),
        ),
        in_specs=[ANY] * 6,
        out_specs=(ANY, VMEM, VMEM, VMEM),
        scratch_shapes=[
            pltpu.VMEM((n_ctx, rows, head), BF16),
            pltpu.VMEM((n_ctx, rows, head), BF16),
            pltpu.VMEM((n_ctx, rows, head), BF16),
            pltpu.VMEM((rows, kv_width), BF16),
            pltpu.VMEM((n_dp, rows, kv_width), BF16),
            pltpu.VMEM((model, kv_width), BF16),
            pltpu.VMEM((n_dp, rows, win), BF16),
            pltpu.VMEM((win, kv_width), F32),
            pltpu.VMEM((n_ctx, pad, kv_width), BF16),
            pltpu.VMEM((n_ctx, pad, kv_width), BF16),
            dma((4, n_ctx)),
            dma((4, n_ctx)),
            dma((6,)),
            dma((n_dp, 3, 2)),
            dma((n_dp, 2)),
            dma((n_ctx,)),
            dma((n_ctx,)),
        ],
        compiler_params=pltpu.CompilerParams(
            collective_id=1, has_side_effects=True, vmem_limit_bytes=32 << 20
        ),
        name="give_back",
    )(gq, gk, gv, ga, w_value, hf)
    return (hidden_grad[None], query_grad[None], key_grad[None], weight_grad)


def solution(mesh):
    rows = P("dp", "ctx", None)
    return jax.shard_map(
        on_device,
        mesh=mesh,
        in_specs=(rows, rows, rows, rows, P(), P(), P(), P("dp", "ctx"), P("dp", "ctx")),
        out_specs=(rows, rows, rows, P(("dp", "ctx"), None)),
        check_vma=False,
    )
```

profile of v0, /device:TPU:25, one launch (start us, length us, event | category | flops | bytes accessed | tf_op | source)
XLA Modules:
  0.0 152.4 jit_solution(13542693291369339648)
XLA Ops:
  0.6 0.7 pad_add_fusion.index
  1.3 0.0 copy-start
  1.3 2.5 %copy-done = bf16[5120,512]{1,0:T(8,128)(2,1)S(1)} copy-done((bf16[5120,512]{1,0:T(8,128)(2,1)S(1)}, bf16[5120,512]{1,0:T(8,128)(2,1)}, u32[]{:S(2)}) %copy-start) | copy-done | bytes 5242904
  3.8 0.0 copy-start.2
  3.8 1.3 copy-done.2
  5.1 0.0 copy-start.3
  5.1 1.2 copy-done.3
  6.3 0.0 copy-start.4
  6.3 1.2 copy-done.4
  7.6 0.0 copy-start.5
  7.6 0.9 copy-done.5
  8.5 0.0 copy-start.6
  8.5 0.0 copy-start.7
  8.5 0.0 copy-start.8
  8.5 0.0 copy-start.9
  8.5 0.0 copy-start.10
  8.5 0.0 copy-start.1
  8.5 54.0 %arrive.1 = (bf16[2048,256]{1,0:T(8,128)(2,1)S(1)}, bf16[2048,256]{1,0:T(8,128)(2,1)S(1)}, bf16[2048,128]{1,0:T(8,128)(2,1)S(1)}, bf16[2048,128]{1,0:T(8,128)(2,...) custom-call(bf16[128,4096]{1,0:T(8,128)(2,1)S(1)} %bitcast.15, bf16[128,4096]{1,0:T(8,128)(2,1)S(1)} %bitcast.16, ...), custom_call_target="tpu_custom_call" | custom-call | tf_op jit(solution)/shard_map/arrive/pallas_call | solution.py:502
  62.5 0.0 copy-done.6
  62.5 0.0 copy-done.7
  62.5 0.0 copy-done.8
  62.5 0.0 copy-done.9
  62.5 0.0 copy-done.10
  62.5 29.0 %attend.1 = (bf16[2048,256]{1,0:T(8,128)(2,1)S(1)}, bf16[2048,128]{1,0:T(8,128)(2,1)S(1)}, bf16[2048,128]{1,0:T(8,128)(2,1)S(1)}, bf16[2048,128]{1,0:T(8,128)(2,1)S(1)}) custom-call(bf16[2048,256]{1,0:T(8,128)(2,1)S(1)} %get-tuple-element.18.q_ref, bf16[2048,256]{1,0:T(8,128)(2,1)S(1)} %get-tuple-element.19.g_ref, ...), custom_call_target="tpu_custom_call" | custom-call | tf_op jit(solution)/shard_map/attend/pallas_call | solution.py:542
  91.5 0.0 copy-done.1
  91.5 57.6 %give_back.1 = (bf16[128,4096]{1,0:T(8,128)(2,1)S(1)}, bf16[128,512]{1,0:T(8,128)(2,1)S(1)}, bf16[128,5120]{1,0:T(8,128)(2,1)S(1)}, f32[20,512]{1,0:T(8,128)S(1)}) custom-call(bf16[2048,256]{1,0:T(8,128)(2,1)S(1)} %get-tuple-element.23.gq, bf16[2048,128]{1,0:T(8,128)(2,1)S(1)} %get-tuple-element.24.gk, bf16[2048,128]{1,0:T(8,128)(2,1)S(1)} %get-tuple-element.25.gv, ...), custom_call_target="tpu_custom_call" | custom-call | tf_op jit(solution)/shard_map/give_back/pallas_call | solution.py:570
  149.1 1.1 copy.21
  150.2 1.0 copy.22
  151.1 0.7 copy.23
  151.8 0.6 copy.24
  (3 shorter events, 0.0 us)
Async XLA Ops:
  1.3 2.5 %copy-start = (bf16[5120,512]{1,0:T(8,128)(2,1)S(1)}, bf16[5120,512]{1,0:T(8,128)(2,1)}, u32[]{:S(2)}) copy-start(bf16[5120,512]{1,0:T(8,128)(2,1)} %w.3) | copy-start | bytes 15728644
  3.8 1.3 copy-start.2
  5.1 1.2 copy-start.3
  6.3 1.2 copy-start.4
  7.6 0.9 copy-start.5
  8.5 54.0 %copy-start.6 = (f32[256,128]{1,0:T(8,128)S(1)}, f32[256,128]{1,0:T(8,128)}, u32[]{:S(2)}) copy-start(f32[256,128]{1,0:T(8,128)} %constant.8.clone.slo_ref) | copy-start | bytes 393220
  8.5 54.0 %copy-start.7 = (f32[256,128]{1,0:T(8,128)S(1)}, f32[256,128]{1,0:T(8,128)}, u32[]{:S(2)}) copy-start(f32[256,128]{1,0:T(8,128)} %constant.7.clone.clo_ref) | copy-start | bytes 393220
  8.5 54.0 %copy-start.8 = (f32[8,128]{1,0:T(8,128)S(1)}, f32[8,128]{1,0:T(8,128)}, u32[]{:S(2)}) copy-start(f32[8,128]{1,0:T(8,128)} %constant.6.clone.fr_ref) | copy-start | bytes 12292
  8.5 54.1 %copy-start.9 = (f32[128]{0:T(128)S(1)}, f32[128]{0:T(128)}, u32[]{:S(2)}) copy-start(f32[128]{0:T(128)} %param.17) | copy-start | bytes 1540
  8.5 54.1 %copy-start.10 = (f32[128]{0:T(128)S(1)}, f32[128]{0:T(128)}, u32[]{:S(2)}) copy-start(f32[128]{0:T(128)} %param.18) | copy-start | bytes 1540
  8.5 83.0 %copy-start.1 = (bf16[5120,512]{1,0:T(8,128)(2,1)S(1)}, bf16[5120,512]{1,0:T(8,128)(2,1)}, u32[]{:S(2)}) copy-start(bf16[5120,512]{1,0:T(8,128)(2,1)} %w.3) | copy-start | bytes 15728644
where the time goes:
time: 153 us; the launch traced here: 152 us
  Pallas kernels  140 us (92%)
  local copies, waits for them, and re-layouts  10.5 us (7%)
    pallas_call x1, Pallas kernels, on_device(): pl.pallas_call(functools.partial(return_kernel, sizes), out_shape=(sds((r...  57.6 us
    pallas_call x1, Pallas kernels, on_device(): pl.pallas_call(functools.partial(arrive_kernel, sizes), out_shape=(sds((s...  54 us
    pallas_call x1, Pallas kernels, on_device(): pl.pallas_call(functools.partial(attend_kernel, (slab, heads, head, 4)),...  29 us
    unnamed x26, local copies, waits for them, and re-layouts  10.5 us

commit v1 on v0

v1 whole, which is shorter than its diff:
```python
import functools
import math

import jax
import jax.numpy as jnp
import numpy as np
from jax import lax
from jax.experimental import pallas as pl
from jax.experimental.pallas import tpu as pltpu
from jax.sharding import PartitionSpec as P

epsilon = 1e-06
rope_base = 1000000.0
BF16, F32, I32 = jnp.bfloat16, jnp.float32, jnp.int32
ANY = pl.BlockSpec(memory_space=pl.ANY)
HBM = pl.BlockSpec(memory_space=pltpu.HBM)
VMEM = pl.BlockSpec(memory_space=pltpu.VMEM)
TILE = 256
NT = (((1,), (1,)), ((), ()))
TN = (((0,), (0,)), ((), ()))


def dot(a, b, dims=(((1,), (0,)), ((), ()))):
    return lax.dot_general(a, b, dims, preferred_element_type=F32)


def send(src, dst, ssem, rsem, dp, ctx):
    return pltpu.make_async_remote_copy(
        src_ref=src,
        dst_ref=dst,
        send_sem=ssem,
        recv_sem=rsem,
        device_id=(dp, ctx),
        device_id_type=pl.DeviceIdType.MESH,
    )


def signal(sem, dp, ctx):
    pl.semaphore_signal(
        sem, inc=1, device_id=(dp, ctx), device_id_type=pl.DeviceIdType.MESH
    )


def window(dp, share):
    return pl.multiple_of((dp * share) // 128 * 128, 128)


def far(d, n_z):
    return n_z == 8 and d in (3, 5)


def arrive_kernel(
    sizes, q, g, k, h, w, index, q_o, g_o, k_o, v_o, index_o, hf_o,
    h_v, w_v, v_v, ssem, rsem, ysem, yrem, isem, irem, hssem, hrsem, lsem,
):
    n_dp, n_x, n_y, rows, width, head, share, win = sizes
    n_ctx, n_z = n_x * n_y, n_dp // 2
    dp, me = lax.axis_index("dp"), lax.axis_index("ctx")
    x, y, z, core = me // n_y, me % n_y, dp // 2, dp % 2

    load_h = pltpu.make_async_copy(h, h_v, lsem.at[0])
    load_w = pltpu.make_async_copy(w, w_v, lsem.at[1])
    load_h.start()
    load_w.start()

    barrier = pltpu.get_barrier_semaphore()

    @pl.loop(1, n_ctx)
    def _(d):
        signal(barrier, dp, lax.rem(me + d, n_ctx))

    @pl.loop(1, n_dp)
    def _(d):
        signal(barrier, lax.rem(dp + d, n_dp), me)

    pl.semaphore_wait(barrier, n_ctx - 1 + n_dp - 1)

    def cols(s, size):
        return pl.ds(pl.multiple_of(s * size, size), size)

    def on_x(kind, d, to, frm):
        src, dst = (
            (k.at[:, cols(to, head)], k_o.at[y, frm]),
            (q.at[:, cols(to, width)], q_o.at[frm]),
            (v_v.at[:, cols(to, head)], v_o.at[y, frm]),
            (g.at[:, cols(to, width)], g_o.at[frm]),
        )[kind]
        if d == 0:
            return pltpu.make_async_copy(src, dst, lsem.at[2 + kind])
        return send(src, dst, ssem.at[kind, d], rsem.at[kind, d], dp, to * n_y + y)

    def on_y(kind, d, to, frm):
        ref = (k_o, v_o)[kind]
        return send(ref.at[frm], ref.at[frm], ysem.at[kind, d], yrem.at[kind, d], dp, x * n_y + to)

    def start_x(kind):
        for d in (*range(1, n_x), 0):
            on_x(kind, d, lax.rem(x + d, n_x), x).start()

    def arrived_x(kind):
        on_x(kind, 0, x, x).wait()
        for d in range(1, n_x):
            on_x(kind, d, x, lax.rem(x + n_x - d, n_x)).wait_recv()

    def start_y(kind):
        for d in range(1, n_y):
            on_y(kind, d, lax.rem(y + d, n_y), y).start()

    def idx_copy(d, to, frm):
        return send(index, index_o.at[frm], isem.at[d], irem.at[d], dp, to)

    def hf_copy(i, to, frm):
        return send(
            h.at[:, pl.ds(window(to, share), win)], hf_o.at[frm], hssem.at[i], hrsem.at[i], to, me
        )

    def hf_pairs():
        for d in range(n_z):
            for c in range(2):
                if (d or c) and not far(d, n_z):
                    flip = (core + c) % 2
                    yield (
                        d * 2 + c,
                        lax.rem(z + d, n_z) * 2 + flip,
                        lax.rem(z + n_z - d, n_z) * 2 + flip,
                    )

    start_x(0)
    start_x(1)

    @pl.loop(1, n_ctx)
    def _(d):
        idx_copy(d, lax.rem(me + d, n_ctx), me).start()

    own_idx = pltpu.make_async_copy(index, index_o.at[me], lsem.at[6])
    own_idx.start()
    for i, to, frm in hf_pairs():
        hf_copy(i, to, dp).start()
    load_h.wait()
    own_hf = pltpu.make_async_copy(
        h_v.at[:, pl.ds(window(dp, share), win)], hf_o.at[dp], lsem.at[7]
    )
    own_hf.start()
    load_w.wait()
    v_v[...] = dot(h_v[...], w_v[...]).astype(BF16)
    start_x(2)
    start_x(3)
    arrived_x(0)
    start_y(0)
    arrived_x(2)
    start_y(1)
    own_idx.wait()
    own_hf.wait()
    arrived_x(1)
    arrived_x(3)
    for kind in range(2):
        for d in range(1, n_y):
            on_y(kind, d, y, lax.rem(y + n_y - d, n_y)).wait_recv()
            on_y(kind, d, lax.rem(y + d, n_y), y).wait_send()
    for kind in range(4):
        for d in range(1, n_x):
            on_x(kind, d, lax.rem(x + d, n_x), x).wait_send()

    @pl.loop(1, n_ctx)
    def _(d):
        idx_copy(d, lax.rem(me + d, n_ctx), me).wait_send()
        idx_copy(d, me, lax.rem(me + n_ctx - d, n_ctx)).wait_recv()

    for i, to, frm in hf_pairs():
        hf_copy(i, to, dp).wait_send()
        hf_copy(i, dp, frm).wait_recv()


def attend_kernel(
    sizes, q_ref, g_ref, k_ref, v_ref, dest_ref, ids_ref, qg_ref, kg_ref, fr_ref, clo_ref, slo_ref,
    gq_ref, gk_ref, gv_ref, ga_ref,
    qs, gs, kn, vs, cs, sn, c0t, s0t, es, ds_, gk_acc, gv_acc, gq_acc,
):
    n_x, n_y, rows, heads, head, n_docs = sizes
    slab = n_x * n_y * rows
    blocks = slab // rows
    tiles = slab // TILE
    factor = head ** (-0.5)
    half = head // 2
    y = lax.axis_index("ctx") % n_y

    ids = ids_ref[...]
    bounds = [jnp.sum((ids < d).astype(F32)).astype(I32) for d in range(1, n_docs)]

    def start_of(row):
        start = jnp.zeros_like(row)
        for b in bounds:
            start = jnp.where(row >= b, b, start)
        return start

    q_gain, k_gain = qg_ref[...], kg_ref[...]
    lane = lax.broadcasted_iota(I32, (1, head), 1)
    sign = jnp.where(lane < half, -1.0, 1.0).astype(F32)

    def normrope(u, gain, c, s):
        inv = lax.rsqrt(jnp.mean(u * u, axis=-1, keepdims=True) + epsilon)
        v = u * inv * gain
        return v * c + pltpu.roll(v, half, 1) * s

    def normrope_back(u, gz, gain, c, s):
        inv = lax.rsqrt(jnp.mean(u * u, axis=-1, keepdims=True) + epsilon)
        hat = u * inv
        gn = (gz * c - pltpu.roll(gz, half, 1) * s) * gain
        return inv * (gn - hat * jnp.mean(gn * hat, axis=-1, keepdims=True))

    line = lax.broadcasted_iota(I32, (blocks * n_docs, 1), 0)
    doc = line % n_docs
    first = jnp.zeros_like(line)
    for d, b in enumerate(bounds):
        first = jnp.where(doc == d + 1, b, first)
    angle = ((line // n_docs) * rows - first).astype(F32) * fr_ref[:1]
    c0t[...] = jnp.cos(angle)
    s0t[...] = jnp.sin(angle)

    def block(i):
        return pl.ds(pl.multiple_of(i * rows, rows), rows)

    @pl.loop(0, blocks)
    def _(i):
        at = block(i)
        row = lax.broadcasted_iota(I32, (rows, 1), 0) + i * rows
        c0 = jnp.broadcast_to(c0t[pl.ds(i * n_docs, 1), :], (rows, head))
        s0 = jnp.broadcast_to(s0t[pl.ds(i * n_docs, 1), :], (rows, head))
        for d, b in enumerate(bounds):
            c0 = jnp.where(row >= b, c0t[pl.ds(i * n_docs + d + 1, 1), :], c0)
            s0 = jnp.where(row >= b, s0t[pl.ds(i * n_docs + d + 1, 1), :], s0)
        clo, slo = clo_ref[...], slo_ref[...]
        c = clo * c0 - slo * s0
        s = (slo * c0 + clo * s0) * sign
        cs[at, :] = c
        sn[at, :] = s
        kn[at, :] = normrope(k_ref[i % n_y, i // n_y].astype(F32), k_gain, c, s).astype(BF16)
        gk_acc[at, :] = jnp.zeros((rows, head), F32)
        gv_acc[at, :] = jnp.zeros((rows, head), F32)

    @pl.loop(0, n_x)
    def _(m):
        at = block(m * n_y + y)
        c, s = cs[at, :], sn[at, :]
        for hd in range(heads):
            lanes = slice(hd * head, (hd + 1) * head)
            to = slice(hd * rows, (hd + 1) * rows)
            u = q_ref[m, :, lanes].astype(F32)
            qs[m, to, :] = normrope(u, q_gain, c, s).astype(BF16)
            gs[m, to, :] = g_ref[m, :, lanes]

    values = v_ref[...].reshape(slab, head)

    @pl.loop(0, tiles)
    def _(i):
        at = pl.ds(pl.multiple_of(i * TILE, TILE), TILE)
        row = lax.broadcasted_iota(I32, (TILE, 1), 0) + i * TILE
        placing = jnp.where(row == dest_ref[...], 1.0, 0.0).astype(BF16)
        vs[at, :] = dot(placing, values).astype(BF16)

    scale = factor * math.log2(math.e)
    part = heads * rows // 2

    @pl.loop(0, n_x)
    def _(m):
        i = m * n_y + y
        r0 = pl.multiple_of(i * rows, rows)
        row = lax.broadcasted_iota(I32, (1, rows), 1) + r0
        start = start_of(row)
        first = jnp.zeros((), I32)
        for b in bounds:
            first = jnp.where(r0 >= b, b, first)
        low, high = first // TILE, (r0 + rows - 1) // TILE + 1

        def forward(j, carry):
            k0 = pl.multiple_of(j * TILE, TILE)
            at = pl.ds(k0, TILE)
            key = lax.broadcasted_iota(I32, (TILE, 1), 0) + k0
            allowed = (key >= start) & (key <= row)
            sums = []
            for n in range(2):
                here = slice(n * part, (n + 1) * part)
                logits = dot(kn[at, :], qs[m, here, :], NT) * scale
                pg = dot(vs[at, :], gs[m, here, :], NT)
                e = jnp.concatenate(
                    [
                        jnp.where(allowed, jnp.exp2(logits[:, c : c + rows]), 0.0)
                        for c in range(0, part, rows)
                    ],
                    axis=1,
                )
                es[j, :, here] = e
                ds_[j, :, here] = pg
                sums.append(carry[2 * n] + jnp.sum(e, axis=0, keepdims=True))
                sums.append(carry[2 * n + 1] + jnp.sum(e * pg, axis=0, keepdims=True))
            return tuple(sums)

        zero = jnp.zeros((1, part), F32)
        sums = lax.fori_loop(low, high, forward, (zero,) * 4)
        inv = [1.0 / sums[0], 1.0 / sums[2]]
        delta = [sums[1] * inv[0], sums[3] * inv[1]]
        gq_acc[...] = jnp.zeros_like(gq_acc)

        @pl.loop(low, high)
        def _(j):
            at = pl.ds(pl.multiple_of(j * TILE, TILE), TILE)
            for n in range(2):
                here = slice(n * part, (n + 1) * part)
                p = es[j, :, here] * inv[n]
                dsj = (p * (ds_[j, :, here] - delta[n])).astype(BF16)
                gk_acc[at, :] += dot(dsj, qs[m, here, :])
                gv_acc[at, :] += dot(p.astype(BF16), gs[m, here, :])
                gq_acc[here, :] += dot(dsj, kn[at, :], TN)

        at = block(i)
        for hd in range(heads):
            lanes = slice(hd * head, (hd + 1) * head)
            gz = gq_acc[hd * rows : (hd + 1) * rows] * factor
            u = q_ref[m, :, lanes].astype(F32)
            gq_ref[m, :, lanes] = normrope_back(u, gz, q_gain, cs[at, :], sn[at, :]).astype(BF16)

    @pl.loop(0, blocks)
    def _(i):
        at = block(i)
        gz = gk_acc[at, :] * factor
        u = k_ref[i % n_y, i // n_y].astype(F32)
        gk_ref[i % n_y, i // n_y] = normrope_back(u, gz, k_gain, cs[at, :], sn[at, :]).astype(BF16)
        gv = gv_acc[at, :].astype(BF16)
        gv_ref[i % n_y, i // n_y] = gv
        vs[at, :] = gv

    @pl.loop(0, blocks)
    def _(i):
        dest = dest_ref[:, block(i)].astype(F32)
        dest = jnp.broadcast_to(dest, (rows, rows)).T
        slot = lax.broadcasted_iota(I32, (1, rows), 1).astype(F32)
        picking = jnp.concatenate(
            [
                jnp.where(dest == slot + float(c * rows), 1.0, 0.0).astype(BF16)
                for c in range(blocks)
            ],
            axis=1,
        )
        ga_ref[i // n_x, i % n_x] = dot(picking, vs[...]).astype(BF16)


def return_kernel(
    sizes, gq, gk, gv, ga, w, h, hf, gq_o, gk_o, h_o, w_o,
    r1, s1, r2, vg, ag, w_v, hf_v, hft, dw, dws, dwr,
    qsem, qrem, ysem, yrem, xsem, xrem, lsem, ag_s, ag_r, ws, wr, hssem, hrsem,
):
    n_dp, n_x, n_y, rows, width, head, share, win = sizes
    n_ctx, n_z = n_x * n_y, n_dp // 2
    dp, me = lax.axis_index("dp"), lax.axis_index("ctx")
    x, y, z, core = me // n_y, me % n_y, dp // 2, dp % 2
    after = lax.rem(z + 1, n_z) * 2 + core
    before = lax.rem(z + n_z - 1, n_z) * 2 + core
    twin = z * 2 + 1 - core
    ahead = n_z // 2
    behind = n_z - 1 - ahead

    load_w = pltpu.make_async_copy(w, w_v, lsem.at[0])
    load_w.start()

    def hf_pairs(away):
        for d in range(n_z):
            for c in range(2):
                if far(d, n_z) == away:
                    flip = (core + c) % 2
                    yield (
                        d * 2 + c,
                        lax.rem(z + d, n_z) * 2 + flip,
                        lax.rem(z + n_z - d, n_z) * 2 + flip,
                    )

    hf_loads = [
        pltpu.make_async_copy(hf.at[frm], hf_v.at[frm], hrsem.at[i])
        for i, _, frm in hf_pairs(False)
    ]
    for copy in hf_loads:
        copy.start()

    barrier = pltpu.get_barrier_semaphore()

    @pl.loop(1, n_ctx)
    def _(d):
        signal(barrier, dp, lax.rem(me + d, n_ctx))

    @pl.loop(1, n_dp)
    def _(d):
        signal(barrier, lax.rem(dp + d, n_dp), me)

    pl.semaphore_wait(barrier, n_ctx - 1 + n_dp - 1)

    grads = (ga, gv, gk)

    def on_y(kind, d, to, frm):
        src, dst = grads[kind].at[to], r1.at[kind, frm]
        if d == 0:
            return pltpu.make_async_copy(src, dst, lsem.at[1 + kind])
        return send(src, dst, ysem.at[kind, d], yrem.at[kind, d], dp, x * n_y + to)

    def on_x(kind, d, to, frm):
        dst = ag.at[dp, frm] if kind == 0 else r2.at[kind - 1, frm]
        return send(s1.at[kind, to], dst, xsem.at[kind, d], xrem.at[kind, d], dp, to * n_y + y)

    def q_copy(n, d, to, frm):
        part = width // 2
        src = gq.at[to, :, pl.ds(n * part, part)]
        dst = gq_o.at[:, pl.ds(pl.multiple_of(frm * width + n * part, part), part)]
        if d == 0:
            return pltpu.make_async_copy(src, dst, lsem.at[4 + n])
        return send(src, dst, qsem.at[n, d], qrem.at[n, d], dp, to * n_y + y)

    def hf_copy(i, to, frm):
        return send(
            h.at[:, pl.ds(window(to, share), win)], hf_v.at[frm], hssem.at[i], hrsem.at[i], to, me
        )

    def start_y(kind):
        for d in (*range(1, n_y), 0):
            on_y(kind, d, lax.rem(y + d, n_y), y).start()

    def start_q(n):
        for d in (*range(1, n_x), 0):
            q_copy(n, d, lax.rem(x + d, n_x), x).start()

    def reduce_y(kind):
        on_y(kind, 0, y, y).wait()
        for d in range(1, n_y):
            on_y(kind, d, y, lax.rem(y + n_y - d, n_y)).wait_recv()
        for m in range(n_x):
            total = r1[kind, 0, m].astype(F32)
            for f in range(1, n_y):
                total = total + r1[kind, f, m].astype(F32)
            s1[kind, m] = total.astype(BF16)

    def start_x(kind):
        for d in range(1, n_x):
            on_x(kind, d, lax.rem(x + d, n_x), x).start()

    def arrived_x(kind):
        for d in range(1, n_x):
            on_x(kind, d, x, lax.rem(x + n_x - d, n_x)).wait_recv()

    start_y(0)
    start_q(0)
    for i, to, frm in hf_pairs(True):
        hf_copy(i, to, dp).start()
    start_y(1)
    start_y(2)

    reduce_y(0)
    start_x(0)
    start_q(1)
    ag[dp, x] = s1[0, x]
    for copy in hf_loads:
        copy.wait()
    for i, _, frm in hf_pairs(False):
        hft[frm] = hf_v[frm].T
    arrived_x(0)
    chunk = n_x // 2

    def piece(slot, ch):
        return ag.at[slot, pl.ds(ch * chunk, chunk)]

    def ring(slot, ch, way, to):
        return send(piece(slot, ch), piece(slot, ch), ag_s.at[slot, way, ch], ag_r.at[slot, ch], to, me)

    sent = []

    def go(slot, ch, way, to):
        copy = ring(slot, ch, way, to)
        copy.start()
        sent.append(copy)

    for ch in range(2):
        if ahead:
            go(dp, ch, 0, after)
        if behind:
            go(dp, ch, 1, before)
    for ch in range(2):
        go(dp, ch, 2, twin)

    reduce_y(1)
    start_x(1)
    reduce_y(2)
    start_x(2)
    load_w.wait()
    r2[0, x] = s1[1, x]
    r2[1, x] = s1[2, x]
    arrived_x(1)
    for hd in range(n_x):
        vg[:, hd * head : (hd + 1) * head] = r2[0, hd]

    model = h_o.shape[1]
    steps = max(ahead, 1)
    span = model // steps
    sub = 256 if span % 256 == 0 else span
    for t in range(1, steps + 1):

        @pl.loop(0, span // sub)
        def _(n, t=t):
            at = pl.ds(pl.multiple_of((t - 1) * span + n * sub, sub), sub)
            h_o[:, at] = dot(vg[...], w_v[at, :], NT).astype(BF16)

        for ch in range(2):
            if t <= ahead:
                slot = lax.rem(z + n_z - t, n_z) * 2 + core
                ring(slot, ch, 0, after).wait_recv()
                if t < ahead:
                    go(slot, ch, 0, after)
                go(slot, ch, 2, twin)
            if t <= behind:
                slot = lax.rem(z + t, n_z) * 2 + core
                ring(slot, ch, 1, before).wait_recv()
                if t < behind:
                    go(slot, ch, 1, before)
                go(slot, ch, 2, twin)
        if t == 1:
            arrived_x(2)
            for hd in range(n_x):
                gk_o[:, hd * head : (hd + 1) * head] = r2[1, hd]
        if t == 2 or t == steps:
            if t == min(2, steps):
                for i, _, frm in hf_pairs(True):
                    hf_copy(i, dp, frm).wait_recv()
                    hft[frm] = hf_v[frm].T

    for t in range(n_z):
        slot = lax.rem(z + t, n_z) * 2 + 1 - core
        for ch in range(2):
            ring(slot, ch, 2, twin).wait_recv()

    group = 4
    for n in range(n_dp // group):
        at = slice(n * group, (n + 1) * group)
        a = jnp.concatenate([hft[e] for e in range(n * group, (n + 1) * group)], axis=1)
        b = jnp.concatenate([ag[at, hd].reshape(group * rows, head) for hd in range(n_x)], axis=1)
        if n == 0:
            dw[...] = dot(a, b)
        else:
            dw[...] += dot(a, b)
    off = pl.multiple_of(dp * share - (dp * share) // 128 * 128, 64)
    out_rows = share // n_ctx
    pad = dws.shape[1]
    for c in range(n_ctx):
        dws[c, :out_rows, :] = dw[pl.ds(off, share), :][c * out_rows : (c + 1) * out_rows].astype(BF16)
        if pad > out_rows:
            dws[c, out_rows:, :] = jnp.zeros((pad - out_rows, n_x * head), BF16)

    def w_copy(d, to, frm):
        return send(dws.at[to], dwr.at[frm], ws.at[d], wr.at[d], dp, to)

    @pl.loop(1, n_ctx)
    def _(d):
        w_copy(d, lax.rem(me + d, n_ctx), me).start()

    dwr[me] = dws[me]
    for n in range(2):
        q_copy(n, 0, x, x).wait()
        for d in range(1, n_x):
            q_copy(n, d, x, lax.rem(x + n_x - d, n_x)).wait_recv()
            q_copy(n, d, lax.rem(x + d, n_x), x).wait_send()
    for copy in sent:
        copy.wait_send()
    for kind in range(3):
        for d in range(1, n_y):
            on_y(kind, d, lax.rem(y + d, n_y), y).wait_send()
        for d in range(1, n_x):
            on_x(kind, d, lax.rem(x + d, n_x), x).wait_send()
    for i, to, _ in hf_pairs(True):
        hf_copy(i, to, dp).wait_send()

    @pl.loop(1, n_ctx)
    def _(d):
        w_copy(d, me, lax.rem(me + n_ctx - d, n_ctx)).wait_recv()

    total = dwr[0].astype(F32)
    for c in range(1, n_ctx):
        total = total + dwr[c].astype(F32)
    w_o[...] = total[:out_rows] * (1.0 / (n_dp * n_ctx))

    @pl.loop(1, n_ctx)
    def _(d):
        w_copy(d, lax.rem(me + d, n_ctx), me).wait_send()


def on_device(hidden, queries, key_states, out_grad, w_value, q_gain, k_gain, dest_rows, doc_ids):
    n_dp, n_ctx = lax.axis_size("dp"), lax.axis_size("ctx")
    rows, model = hidden.shape[1:]
    head = q_gain.shape[0]
    kv_width = key_states.shape[2]
    n_x = kv_width // head
    n_y = n_ctx // n_x
    width = queries.shape[2] // n_x
    heads = width // head
    slab = rows * n_ctx
    share = model // n_dp
    win = (share + 127) // 128 * 128
    sizes = (n_dp, n_x, n_y, rows, width, head, share, win)
    sds = jax.ShapeDtypeStruct
    dma = pltpu.SemaphoreType.DMA

    index = jnp.concatenate([dest_rows, doc_ids], axis=0)
    wide = sds((n_x, rows, width), BF16)
    narrow = sds((n_y, n_x, rows, head), BF16)
    q_in, g_in, k_in, v_in, index_in, hf = pl.pallas_call(
        functools.partial(arrive_kernel, sizes),
        out_shape=(
            wide,
            wide,
            narrow,
            narrow,
            sds((n_ctx, 2, rows), I32),
            sds((n_dp, rows, win), BF16),
        ),
        in_specs=[HBM] * 5 + [ANY],
        out_specs=(ANY,) * 6,
        scratch_shapes=[
            pltpu.VMEM((rows, model), BF16),
            pltpu.VMEM((model, kv_width), BF16),
            pltpu.VMEM((rows, kv_width), BF16),
            dma((4, n_x)),
            dma((4, n_x)),
            dma((2, n_y)),
            dma((2, n_y)),
            dma((n_ctx,)),
            dma((n_ctx,)),
            dma((n_dp,)),
            dma((n_dp,)),
            dma((8,)),
        ],
        compiler_params=pltpu.CompilerParams(
            collective_id=0, has_side_effects=True, vmem_limit_bytes=16 << 20
        ),
        name="arrive",
    )(*[pltpu.with_memory_space_constraint(a, pltpu.HBM) for a in (queries[0], out_grad[0], key_states[0], hidden[0], w_value)], index)

    dest_all = index_in[:, 0].reshape(n_x, n_y, rows).transpose(1, 0, 2).reshape(1, slab)
    ids_all = index_in[:, 1]
    half = head // 2
    frequency = rope_base ** (-(np.arange(half, dtype=np.float64) * 2.0 / head))
    frequency = np.concatenate([frequency, frequency])[None]
    low = np.arange(rows, dtype=np.float64)[:, None] * frequency
    consts = [
        jnp.asarray(np.broadcast_to(frequency, (8, head)), F32),
        jnp.asarray(np.cos(low), F32),
        jnp.asarray(np.sin(low), F32),
    ]
    tiles = slab // TILE
    n_docs = 4
    gq, gk, gv, ga = pl.pallas_call(
        functools.partial(attend_kernel, (n_x, n_y, rows, heads, head, n_docs)),
        out_shape=(wide, narrow, narrow, narrow),
        in_specs=[VMEM] * 11,
        out_specs=(VMEM,) * 4,
        scratch_shapes=[
            pltpu.VMEM((n_x, heads * rows, head), BF16),
            pltpu.VMEM((n_x, heads * rows, head), BF16),
            pltpu.VMEM((slab, head), BF16),
            pltpu.VMEM((slab, head), BF16),
            pltpu.VMEM((slab, head), F32),
            pltpu.VMEM((slab, head), F32),
            pltpu.VMEM((n_ctx * n_docs, head), F32),
            pltpu.VMEM((n_ctx * n_docs, head), F32),
            pltpu.VMEM((tiles, TILE, heads * rows), F32),
            pltpu.VMEM((tiles, TILE, heads * rows), F32),
            pltpu.VMEM((slab, head), F32),
            pltpu.VMEM((slab, head), F32),
            pltpu.VMEM((heads * rows, head), F32),
        ],
        compiler_params=pltpu.CompilerParams(vmem_limit_bytes=44 << 20),
        name="attend",
    )(q_in, g_in, k_in, v_in, dest_all, ids_all, q_gain[None], k_gain[None], *consts)

    out_rows = share // n_ctx
    pad = (out_rows + 15) // 16 * 16
    query_grad, key_grad, hidden_grad, weight_grad = pl.pallas_call(
        functools.partial(return_kernel, sizes),
        out_shape=(
            sds((rows, n_x * width), BF16),
            sds((rows, kv_width), BF16),
            sds((rows, model), BF16),
            sds((out_rows, kv_width), F32),
        ),
        in_specs=[ANY] * 4 + [HBM] * 2 + [ANY],
        out_specs=(ANY, VMEM, VMEM, VMEM),
        scratch_shapes=[
            pltpu.VMEM((3, n_y, n_x, rows, head), BF16),
            pltpu.VMEM((3, n_x, rows, head), BF16),
            pltpu.VMEM((2, n_x, rows, head), BF16),
            pltpu.VMEM((rows, kv_width), BF16),
            pltpu.VMEM((n_dp, n_x, rows, head), BF16),
            pltpu.VMEM((model, kv_width), BF16),
            pltpu.VMEM((n_dp, rows, win), BF16),
            pltpu.VMEM((n_dp, win, rows), BF16),
            pltpu.VMEM((win, kv_width), F32),
            pltpu.VMEM((n_ctx, pad, kv_width), BF16),
            pltpu.VMEM((n_ctx, pad, kv_width), BF16),
            dma((2, n_x)),
            dma((2, n_x)),
            dma((3, n_y)),
            dma((3, n_y)),
            dma((3, n_x)),
            dma((3, n_x)),
            dma((6,)),
            dma((n_dp, 3, 2)),
            dma((n_dp, 2)),
            dma((n_ctx,)),
            dma((n_ctx,)),
            dma((n_dp,)),
            dma((n_dp,)),
        ],
        compiler_params=pltpu.CompilerParams(
            collective_id=1, has_side_effects=True, vmem_limit_bytes=32 << 20
        ),
        name="give_back",
    )(gq, gk, gv, ga, w_value, hidden[0], hf)
    return (hidden_grad[None], query_grad[None], key_grad[None], weight_grad)


def solution(mesh):
    rows = P("dp", "ctx", None)
    return jax.shard_map(
        on_device,
        mesh=mesh,
        in_specs=(rows, rows, rows, rows, P(), P(), P(), P("dp", "ctx"), P("dp", "ctx")),
        out_specs=(rows, rows, rows, P(("dp", "ctx"), None)),
        check_vma=False,
    )
```

time: 153 us -> 132 us (0.86)
  Pallas kernels: 140 us -> 128 us
  local copies, waits for them, and re-layouts: 10.5 us -> 3.36 us
    pallas_call x2, Pallas kernels: 82.9 us -> 72.4 us  [the longest x1 38.4 us: on_device(): pl.pallas_call(functools.partial(arrive_kernel, sizes), out_shape=(wide,...]
    unnamed x26 -> x18, local copies, waits for them, and re-layouts: 10.5 us -> 3.34 us
    pallas_call x1, Pallas kernels: 57.6 us -> 55.5 us  [on_device(): pl.pallas_call(functools.partial(return_kernel, sizes), out_shape=(sds((r...]
where the time goes in v1:
time: 132 us; the launch traced here: 133 us
  Pallas kernels  128 us (97%)
  local copies, waits for them, and re-layouts  3.36 us (3%)
    pallas_call x1, Pallas kernels, on_device(): pl.pallas_call(functools.partial(return_kernel, sizes), out_shape=(sds((r...  55.5 us
    pallas_call x1, Pallas kernels, on_device(): pl.pallas_call(functools.partial(arrive_kernel, sizes), out_shape=(wide,...  38.4 us
    pallas_call x1, Pallas kernels, on_device(): pl.pallas_call(functools.partial(attend_kernel, (n_x, n_y, rows, heads, h...  34 us
    unnamed x18, local copies, waits for them, and re-layouts  3.34 us

profile of v1, /device:TPU:25, one launch (start us, length us, event | category | flops | bytes accessed | tf_op | source)
XLA Modules:
  0.0 132.8 jit_solution(435703310077408008)
XLA Ops:
  0.6 0.7 pad_add_fusion.index
  1.3 0.0 copy-start.2
  1.3 0.0 copy-start.3
  1.3 0.0 copy-start.4
  1.3 0.0 copy-start.5
  1.3 0.0 copy-start.6
  1.4 0.0 copy-start
  1.4 38.4 %arrive.1 = (bf16[4,128,1024]{2,1,0:T(8,128)(2,1)S(1)}, bf16[4,128,1024]{2,1,0:T(8,128)(2,1)S(1)}, bf16[4,4,128,128]{3,2,1,0:T(8,128)(2,1)S(1)}, bf16[4,4,128,12...) custom-call(bf16[128,4096]{1,0:T(8,128)(2,1)} %bitcast.23, ...), custom_call_target="tpu_custom_call" | custom-call | tf_op jit(solution)/shard_map/arrive/pallas_call | solution.py:608
  39.8 0.0 copy-done.2
  39.8 0.0 copy-done.3
  39.9 0.0 copy-done.4
  39.9 0.0 copy-done.5
  39.9 0.0 copy-done.6
  39.9 0.0 copy-start.1
  39.9 34.0 %attend.1 = (bf16[4,128,1024]{2,1,0:T(8,128)(2,1)S(1)}, bf16[4,4,128,128]{3,2,1,0:T(8,128)(2,1)S(1)}, bf16[4,4,128,128]{3,2,1,0:T(8,128)(2,1)S(1)}, bf16[4,4,128,128]{3,2,1,0:T(8,128)(2,1)S(1)}) custom-call(bf16[4,128,1024]{2,1,0:T(8,128)(2,1)S(1)} %get-tuple-element.18.q_ref, bf16[4,128,1024]{2,1,0:T(8,128)(2,1)S(1)} %get-tuple-element.19.g_ref, ...), custom_call_target="tpu_custom_call" | custom-call | tf_op jit(solution)/shard_map/attend/pallas_call | solution.py:653
  73.9 0.0 copy-done
  73.9 0.0 copy-done.1
  73.9 55.5 %give_back.1 = (bf16[128,4096]{1,0:T(8,128)(2,1)S(1)}, bf16[128,512]{1,0:T(8,128)(2,1)S(1)}, bf16[128,5120]{1,0:T(8,128)(2,1)S(1)}, f32[20,512]{1,0:T(8,128)S(1)}) custom-call(bf16[4,128,1024]{2,1,0:T(8,128)(2,1)S(1)} %get-tuple-element.23.gq, bf16[4,4,128,128]{3,2,1,0:T(8,128)(2,1)S(1)} %get-tuple-element.24.gk, ...), custom_call_target="tpu_custom_call" | custom-call | tf_op jit(solution)/shard_map/give_back/pallas_call | solution.py:679
  129.5 1.1 copy.22
  130.6 1.0 copy.23
  131.5 0.7 copy.24
  132.2 0.6 copy.25
  (4 shorter events, 0.0 us)
Async XLA Ops:
  1.3 38.5 %copy-start.2 = (f32[128,128]{1,0:T(8,128)S(1)}, f32[128,128]{1,0:T(8,128)}, u32[]{:S(2)}) copy-start(f32[128,128]{1,0:T(8,128)} %constant.8.clone.slo_ref) | copy-start | bytes 196612
  1.3 38.5 %copy-start.3 = (f32[128,128]{1,0:T(8,128)S(1)}, f32[128,128]{1,0:T(8,128)}, u32[]{:S(2)}) copy-start(f32[128,128]{1,0:T(8,128)} %constant.7.clone.clo_ref) | copy-start | bytes 196612
  1.3 38.5 %copy-start.4 = (f32[8,128]{1,0:T(8,128)S(1)}, f32[8,128]{1,0:T(8,128)}, u32[]{:S(2)}) copy-start(f32[8,128]{1,0:T(8,128)} %constant.6.clone.fr_ref) | copy-start | bytes 12292
  1.3 38.5 %copy-start.5 = (f32[128]{0:T(128)S(1)}, f32[128]{0:T(128)}, u32[]{:S(2)}) copy-start(f32[128]{0:T(128)} %param.17) | copy-start | bytes 1540
  1.3 38.5 %copy-start.6 = (f32[128]{0:T(128)S(1)}, f32[128]{0:T(128)}, u32[]{:S(2)}) copy-start(f32[128]{0:T(128)} %param.18) | copy-start | bytes 1540
  1.4 72.6 %copy-start = (bf16[5120,512]{1,0:T(8,128)(2,1)S(1)}, bf16[5120,512]{1,0:T(8,128)(2,1)}, u32[]{:S(2)}) copy-start(bf16[5120,512]{1,0:T(8,128)(2,1)} %w.3) | copy-start | bytes 15728644
  39.9 34.1 %copy-start.1 = (bf16[1,128,5120]{2,1,0:T(8,128)(2,1)S(1)}, bf16[1,128,5120]{2,1,0:T(8,128)(2,1)}, u32[]{:S(2)}) copy-start(bf16[1,128,5120]{2,1,0:T(8,128)(2,1)} %param.12) | copy-start | bytes 3932164

commit v2 on v1

--- a/solution.py
+++ b/solution.py
@@ -45,13 +45,32 @@
     return pl.multiple_of((dp * share) // 128 * 128, 128)
 
 
+def head_lanes(head):
+    lane = lax.broadcasted_iota(I32, (1, head), 1)
+    return jnp.where(lane < head // 2, -1.0, 1.0).astype(F32)
+
+
+def normrope(u, gain, c, s):
+    inv = lax.rsqrt(jnp.mean(u * u, axis=-1, keepdims=True) + epsilon)
+    v = u * inv * gain
+    return v * c + pltpu.roll(v, u.shape[-1] // 2, 1) * s
+
+
+def normrope_back(u, gz, gain, c, s):
+    inv = lax.rsqrt(jnp.mean(u * u, axis=-1, keepdims=True) + epsilon)
+    hat = u * inv
+    gn = (gz * c - pltpu.roll(gz, u.shape[-1] // 2, 1) * s) * gain
+    return inv * (gn - hat * jnp.mean(gn * hat, axis=-1, keepdims=True))
+
+
 def far(d, n_z):
     return n_z == 8 and d in (3, 5)
 
 
 def arrive_kernel(
-    sizes, q, g, k, h, w, index, q_o, g_o, k_o, v_o, index_o, hf_o,
-    h_v, w_v, v_v, ssem, rsem, ysem, yrem, isem, irem, hssem, hrsem, lsem,
+    sizes, q, g, k, h, w, index, qg_ref, kg_ref, fr_ref, clo_ref, slo_ref,
+    q_o, g_o, k_o, index_o, hf_o, cs, sn, kn, qs, vs,
+    h_v, w_v, v_v, v_o, c0t, s0t, ssem, rsem, ysem, yrem, isem, irem, hssem, hrsem, lsem,
 ):
     n_dp, n_x, n_y, rows, width, head, share, win = sizes
     n_ctx, n_z = n_x * n_y, n_dp // 2
@@ -147,68 +166,20 @@
     start_x(3)
     arrived_x(0)
     start_y(0)
-    arrived_x(2)
-    start_y(1)
+
+    @pl.loop(1, n_ctx)
+    def _(d):
+        idx_copy(d, me, lax.rem(me + n_ctx - d, n_ctx)).wait_recv()
+
     own_idx.wait()
-    own_hf.wait()
-    arrived_x(1)
-    arrived_x(3)
-    for kind in range(2):
-        for d in range(1, n_y):
-            on_y(kind, d, y, lax.rem(y + n_y - d, n_y)).wait_recv()
-            on_y(kind, d, lax.rem(y + d, n_y), y).wait_send()
-    for kind in range(4):
-        for d in range(1, n_x):
-            on_x(kind, d, lax.rem(x + d, n_x), x).wait_send()
-
-    @pl.loop(1, n_ctx)
-    def _(d):
-        idx_copy(d, lax.rem(me + d, n_ctx), me).wait_send()
-        idx_copy(d, me, lax.rem(me + n_ctx - d, n_ctx)).wait_recv()
-
-    for i, to, frm in hf_pairs():
-        hf_copy(i, to, dp).wait_send()
-        hf_copy(i, dp, frm).wait_recv()
-
-
-def attend_kernel(
-    sizes, q_ref, g_ref, k_ref, v_ref, dest_ref, ids_ref, qg_ref, kg_ref, fr_ref, clo_ref, slo_ref,
-    gq_ref, gk_ref, gv_ref, ga_ref,
-    qs, gs, kn, vs, cs, sn, c0t, s0t, es, ds_, gk_acc, gv_acc, gq_acc,
-):
-    n_x, n_y, rows, heads, head, n_docs = sizes
-    slab = n_x * n_y * rows
-    blocks = slab // rows
-    tiles = slab // TILE
-    factor = head ** (-0.5)
-    half = head // 2
-    y = lax.axis_index("ctx") % n_y
-
-    ids = ids_ref[...]
-    bounds = [jnp.sum((ids < d).astype(F32)).astype(I32) for d in range(1, n_docs)]
-
-    def start_of(row):
-        start = jnp.zeros_like(row)
-        for b in bounds:
-            start = jnp.where(row >= b, b, start)
-        return start
-
-    q_gain, k_gain = qg_ref[...], kg_ref[...]
-    lane = lax.broadcasted_iota(I32, (1, head), 1)
-    sign = jnp.where(lane < half, -1.0, 1.0).astype(F32)
-
-    def normrope(u, gain, c, s):
-        inv = lax.rsqrt(jnp.mean(u * u, axis=-1, keepdims=True) + epsilon)
-        v = u * inv * gain
-        return v * c + pltpu.roll(v, half, 1) * s
-
-    def normrope_back(u, gz, gain, c, s):
-        inv = lax.rsqrt(jnp.mean(u * u, axis=-1, keepdims=True) + epsilon)
-        hat = u * inv
-        gn = (gz * c - pltpu.roll(gz, half, 1) * s) * gain
-        return inv * (gn - hat * jnp.mean(gn * hat, axis=-1, keepdims=True))
-
-    line = lax.broadcasted_iota(I32, (blocks * n_docs, 1), 0)
+
+    n_docs = c0t.shape[0] // n_ctx
+    ids = index_o[:, 1, :]
+    bounds = [
+        jnp.sum(jnp.sum((ids < d).astype(F32), axis=1, keepdims=True), axis=0, keepdims=True).astype(I32)
+        for d in range(1, n_docs)
+    ]
+    line = lax.broadcasted_iota(I32, (n_ctx * n_docs, 1), 0)
     doc = line % n_docs
     first = jnp.zeros_like(line)
     for d, b in enumerate(bounds):
@@ -216,11 +187,12 @@
     angle = ((line // n_docs) * rows - first).astype(F32) * fr_ref[:1]
     c0t[...] = jnp.cos(angle)
     s0t[...] = jnp.sin(angle)
+    sign = head_lanes(head)
 
     def block(i):
         return pl.ds(pl.multiple_of(i * rows, rows), rows)
 
-    @pl.loop(0, blocks)
+    @pl.loop(0, n_ctx)
     def _(i):
         at = block(i)
         row = lax.broadcasted_iota(I32, (rows, 1), 0) + i * rows
@@ -230,33 +202,90 @@
             c0 = jnp.where(row >= b, c0t[pl.ds(i * n_docs + d + 1, 1), :], c0)
             s0 = jnp.where(row >= b, s0t[pl.ds(i * n_docs + d + 1, 1), :], s0)
         clo, slo = clo_ref[...], slo_ref[...]
-        c = clo * c0 - slo * s0
-        s = (slo * c0 + clo * s0) * sign
-        cs[at, :] = c
-        sn[at, :] = s
-        kn[at, :] = normrope(k_ref[i % n_y, i // n_y].astype(F32), k_gain, c, s).astype(BF16)
-        gk_acc[at, :] = jnp.zeros((rows, head), F32)
-        gv_acc[at, :] = jnp.zeros((rows, head), F32)
+        cs[at, :] = clo * c0 - slo * s0
+        sn[at, :] = (slo * c0 + clo * s0) * sign
+
+    arrived_x(1)
 
     @pl.loop(0, n_x)
     def _(m):
         at = block(m * n_y + y)
         c, s = cs[at, :], sn[at, :]
-        for hd in range(heads):
-            lanes = slice(hd * head, (hd + 1) * head)
-            to = slice(hd * rows, (hd + 1) * rows)
-            u = q_ref[m, :, lanes].astype(F32)
-            qs[m, to, :] = normrope(u, q_gain, c, s).astype(BF16)
-            gs[m, to, :] = g_ref[m, :, lanes]
-
-    values = v_ref[...].reshape(slab, head)
-
-    @pl.loop(0, tiles)
+        for hd in range(width // head):
+            u = q_o[m, :, hd * head : (hd + 1) * head].astype(F32)
+            qs[m, hd * rows : (hd + 1) * rows, :] = normrope(u, qg_ref[...], c, s).astype(BF16)
+
+    arrived_x(2)
+    start_y(1)
+    for d in range(1, n_y):
+        on_y(0, d, y, lax.rem(y + n_y - d, n_y)).wait_recv()
+
+    @pl.loop(0, n_ctx)
+    def _(i):
+        at = block(i)
+        u = k_o[i % n_y, i // n_y].astype(F32)
+        kn[at, :] = normrope(u, kg_ref[...], cs[at, :], sn[at, :]).astype(BF16)
+
+    for d in range(1, n_y):
+        on_y(1, d, y, lax.rem(y + n_y - d, n_y)).wait_recv()
+    dest = jnp.concatenate(
+        [index_o[m * n_y + f, :1, :] for f in range(n_y) for m in range(n_x)], axis=1
+    )
+    slab = n_ctx * rows
+
+    @pl.loop(0, slab // TILE)
     def _(i):
         at = pl.ds(pl.multiple_of(i * TILE, TILE), TILE)
         row = lax.broadcasted_iota(I32, (TILE, 1), 0) + i * TILE
-        placing = jnp.where(row == dest_ref[...], 1.0, 0.0).astype(BF16)
-        vs[at, :] = dot(placing, values).astype(BF16)
+        placing = jnp.where(row == dest, 1.0, 0.0).astype(BF16)
+        vs[at, :] = dot(placing, v_o[...].reshape(slab, head)).astype(BF16)
+
+    own_hf.wait()
+    arrived_x(3)
+    for kind in range(2):
+        for d in range(1, n_y):
+            on_y(kind, d, lax.rem(y + d, n_y), y).wait_send()
+    for kind in range(4):
+        for d in range(1, n_x):
+            on_x(kind, d, lax.rem(x + d, n_x), x).wait_send()
+
+    @pl.loop(1, n_ctx)
+    def _(d):
+        idx_copy(d, lax.rem(me + d, n_ctx), me).wait_send()
+
+    for i, to, frm in hf_pairs():
+        hf_copy(i, to, dp).wait_send()
+        hf_copy(i, dp, frm).wait_recv()
+
+
+def attend_kernel(
+    sizes, qs, g_ref, kn, vs, index_ref,
+    gq_ref, gk_ref, gv_ref, ga_ref,
+    gs, es, ds_, gv_acc, gvt,
+):
+    n_x, n_y, rows, heads, head, n_docs = sizes
+    slab = n_x * n_y * rows
+    blocks = slab // rows
+    factor = head ** (-0.5)
+    y = lax.axis_index("ctx") % n_y
+
+    ids = index_ref[:, 1, :]
+    bounds = [jnp.sum((ids < d).astype(F32)).astype(I32) for d in range(1, n_docs)]
+
+    def start_of(row):
+        start = jnp.zeros_like(row)
+        for b in bounds:
+            start = jnp.where(row >= b, b, start)
+        return start
+
+    def block(i):
+        return pl.ds(pl.multiple_of(i * rows, rows), rows)
+
+    gk_ref[...] = jnp.zeros_like(gk_ref)
+    gv_acc[...] = jnp.zeros_like(gv_acc)
+    for m in range(n_x):
+        for hd in range(heads):
+            gs[m, hd * rows : (hd + 1) * rows, :] = g_ref[m, :, hd * head : (hd + 1) * head]
 
     scale = factor * math.log2(math.e)
     part = heads * rows // 2
@@ -299,7 +328,7 @@
         sums = lax.fori_loop(low, high, forward, (zero,) * 4)
         inv = [1.0 / sums[0], 1.0 / sums[2]]
         delta = [sums[1] * inv[0], sums[3] * inv[1]]
-        gq_acc[...] = jnp.zeros_like(gq_acc)
+        gq_ref[m] = jnp.zeros((heads * rows, head), F32)
 
         @pl.loop(low, high)
         def _(j):
@@ -308,45 +337,32 @@
                 here = slice(n * part, (n + 1) * part)
                 p = es[j, :, here] * inv[n]
                 dsj = (p * (ds_[j, :, here] - delta[n])).astype(BF16)
-                gk_acc[at, :] += dot(dsj, qs[m, here, :])
+                gk_ref[at, :] += dot(dsj, qs[m, here, :])
                 gv_acc[at, :] += dot(p.astype(BF16), gs[m, here, :])
-                gq_acc[here, :] += dot(dsj, kn[at, :], TN)
-
-        at = block(i)
-        for hd in range(heads):
-            lanes = slice(hd * head, (hd + 1) * head)
-            gz = gq_acc[hd * rows : (hd + 1) * rows] * factor
-            u = q_ref[m, :, lanes].astype(F32)
-            gq_ref[m, :, lanes] = normrope_back(u, gz, q_gain, cs[at, :], sn[at, :]).astype(BF16)
+                gq_ref[m, here, :] += dot(dsj, kn[at, :], TN)
 
     @pl.loop(0, blocks)
     def _(i):
-        at = block(i)
-        gz = gk_acc[at, :] * factor
-        u = k_ref[i % n_y, i // n_y].astype(F32)
-        gk_ref[i % n_y, i // n_y] = normrope_back(u, gz, k_gain, cs[at, :], sn[at, :]).astype(BF16)
-        gv = gv_acc[at, :].astype(BF16)
-        gv_ref[i % n_y, i // n_y] = gv
-        vs[at, :] = gv
-
-    @pl.loop(0, blocks)
-    def _(i):
-        dest = dest_ref[:, block(i)].astype(F32)
-        dest = jnp.broadcast_to(dest, (rows, rows)).T
-        slot = lax.broadcasted_iota(I32, (1, rows), 1).astype(F32)
-        picking = jnp.concatenate(
-            [
-                jnp.where(dest == slot + float(c * rows), 1.0, 0.0).astype(BF16)
-                for c in range(blocks)
-            ],
-            axis=1,
-        )
-        ga_ref[i // n_x, i % n_x] = dot(picking, vs[...]).astype(BF16)
+        gv = gv_acc[block(i), :]
+        gv_ref[i % n_y, i // n_y] = gv.astype(BF16)
+        gvt[:, block(i)] = gv.T.astype(BF16)
+
+    for f in range(n_y):
+        for m in range(0, n_x, 2):
+            dest = jnp.concatenate(
+                [index_ref[(m + n) * n_y + f, :1, :] for n in range(2)], axis=1
+            )
+            row = lax.broadcasted_iota(I32, (slab, 1), 0)
+            picking = jnp.where(row == dest, 1.0, 0.0).astype(BF16)
+            moved = dot(gvt[...], picking).T.astype(BF16)
+            for n in range(2):
+                ga_ref[f, m + n] = moved[n * rows : (n + 1) * rows]
 
 
 def return_kernel(
-    sizes, gq, gk, gv, ga, w, h, hf, gq_o, gk_o, h_o, w_o,
-    r1, s1, r2, vg, ag, w_v, hf_v, hft, dw, dws, dwr,
+    sizes, gq_raw, gk_raw, gv, ga, w, h, hf, q_in, k_in, cs, sn, qg_ref, kg_ref,
+    gq_o, gk_o, h_o, w_o,
+    gq, gk, r1, s1, r2, vg, ag, w_v, hf_v, hft, dw, dws, dwr,
     qsem, qrem, ysem, yrem, xsem, xrem, lsem, ag_s, ag_r, ws, wr, hssem, hrsem,
 ):
     n_dp, n_x, n_y, rows, width, head, share, win = sizes
@@ -444,14 +460,33 @@
             on_x(kind, d, x, lax.rem(x + n_x - d, n_x)).wait_recv()
 
     start_y(0)
-    start_q(0)
     for i, to, frm in hf_pairs(True):
         hf_copy(i, to, dp).start()
+    factor = head ** (-0.5)
+
+    @pl.loop(0, n_x)
+    def _(m):
+        at = pl.ds(pl.multiple_of((m * n_y + y) * rows, rows), rows)
+        c, s = cs[at, :], sn[at, :]
+        for hd in range(width // head):
+            lanes = slice(hd * head, (hd + 1) * head)
+            gz = gq_raw[m, hd * rows : (hd + 1) * rows, :] * factor
+            u = q_in[m, :, lanes].astype(F32)
+            gq[m, :, lanes] = normrope_back(u, gz, qg_ref[...], c, s).astype(BF16)
+
+    start_q(0)
     start_y(1)
-    start_y(2)
+
+    @pl.loop(0, n_ctx)
+    def _(i):
+        at = pl.ds(pl.multiple_of(i * rows, rows), rows)
+        gz = gk_raw[at, :] * factor
+        u = k_in[i % n_y, i // n_y].astype(F32)
+        gk[i % n_y, i // n_y] = normrope_back(u, gz, kg_ref[...], cs[at, :], sn[at, :]).astype(BF16)
 
     reduce_y(0)
     start_x(0)
+    start_y(2)
     start_q(1)
     ag[dp, x] = s1[0, x]
     for copy in hf_loads:
@@ -459,10 +494,12 @@
     for i, _, frm in hf_pairs(False):
         hft[frm] = hf_v[frm].T
     arrived_x(0)
-    chunk = n_x // 2
 
     def piece(slot, ch):
-        return ag.at[slot, pl.ds(ch * chunk, chunk)]
+        return ag.at[slot, ch]
+
+    def takes(t, ch, way):
+        return t <= behind or (t == ahead and (ch < n_x // 2) == (way == 0))
 
     def ring(slot, ch, way, to):
         return send(piece(slot, ch), piece(slot, ch), ag_s.at[slot, way, ch], ag_r.at[slot, ch], to, me)
@@ -474,12 +511,12 @@
         copy.start()
         sent.append(copy)
 
-    for ch in range(2):
-        if ahead:
+    for ch in range(n_x):
+        if takes(1, ch, 0):
             go(dp, ch, 0, after)
-        if behind:
+        if takes(1, ch, 1):
             go(dp, ch, 1, before)
-    for ch in range(2):
+    for ch in range(n_x):
         go(dp, ch, 2, twin)
 
     reduce_y(1)
@@ -504,19 +541,14 @@
             at = pl.ds(pl.multiple_of((t - 1) * span + n * sub, sub), sub)
             h_o[:, at] = dot(vg[...], w_v[at, :], NT).astype(BF16)
 
-        for ch in range(2):
-            if t <= ahead:
-                slot = lax.rem(z + n_z - t, n_z) * 2 + core
-                ring(slot, ch, 0, after).wait_recv()
-                if t < ahead:
-                    go(slot, ch, 0, after)
-                go(slot, ch, 2, twin)
-            if t <= behind:
-                slot = lax.rem(z + t, n_z) * 2 + core
-                ring(slot, ch, 1, before).wait_recv()
-                if t < behind:
-                    go(slot, ch, 1, before)
-                go(slot, ch, 2, twin)
+        for ch in range(n_x):
+            for way, to, hop in ((0, after, n_z - t), (1, before, t)):
+                if takes(t, ch, way):
+                    slot = lax.rem(z + hop, n_z) * 2 + core
+                    ring(slot, ch, way, to).wait_recv()
+                    if takes(t + 1, ch, way):
+                        go(slot, ch, way, to)
+                    go(slot, ch, 2, twin)
         if t == 1:
             arrived_x(2)
             for hd in range(n_x):
@@ -529,7 +561,7 @@
 
     for t in range(n_z):
         slot = lax.rem(z + t, n_z) * 2 + 1 - core
-        for ch in range(2):
+        for ch in range(n_x):
             ring(slot, ch, 2, twin).wait_recv()
 
     group = 4
@@ -605,22 +637,45 @@
     index = jnp.concatenate([dest_rows, doc_ids], axis=0)
     wide = sds((n_x, rows, width), BF16)
     narrow = sds((n_y, n_x, rows, head), BF16)
-    q_in, g_in, k_in, v_in, index_in, hf = pl.pallas_call(
+    half = head // 2
+    frequency = rope_base ** (-(np.arange(half, dtype=np.float64) * 2.0 / head))
+    frequency = np.concatenate([frequency, frequency])[None]
+    low = np.arange(rows, dtype=np.float64)[:, None] * frequency
+    consts = [
+        jnp.asarray(np.broadcast_to(frequency, (8, head)), F32),
+        jnp.asarray(np.cos(low), F32),
+        jnp.asarray(np.sin(low), F32),
+    ]
+    n_docs = 4
+    stacked = (n_x, heads * rows, head)
+    flat = sds((slab, head), BF16)
+    kept = [
+        pltpu.with_memory_space_constraint(a, pltpu.HBM)
+        for a in (queries[0], out_grad[0], key_states[0], hidden[0], w_value)
+    ]
+    q_in, g_in, k_in, index_in, hf, cs, sn, kn, qs, vs = pl.pallas_call(
         functools.partial(arrive_kernel, sizes),
         out_shape=(
             wide,
             wide,
             narrow,
-            narrow,
             sds((n_ctx, 2, rows), I32),
             sds((n_dp, rows, win), BF16),
+            sds((slab, head), F32),
+            sds((slab, head), F32),
+            flat,
+            sds(stacked, BF16),
+            flat,
         ),
-        in_specs=[HBM] * 5 + [ANY],
-        out_specs=(ANY,) * 6,
+        in_specs=[HBM] * 5 + [ANY] + [VMEM] * 5,
+        out_specs=(VMEM, ANY, VMEM, VMEM, ANY) + (VMEM,) * 5,
         scratch_shapes=[
             pltpu.VMEM((rows, model), BF16),
             pltpu.VMEM((model, kv_width), BF16),
             pltpu.VMEM((rows, kv_width), BF16),
+            pltpu.VMEM((n_y, n_x, rows, head), BF16),
+            pltpu.VMEM((n_ctx * n_docs, head), F32),
+            pltpu.VMEM((n_ctx * n_docs, head), F32),
             dma((4, n_x)),
             dma((4, n_x)),
             dma((2, n_y)),
@@ -632,47 +687,27 @@
             dma((8,)),
         ],
         compiler_params=pltpu.CompilerParams(
-            collective_id=0, has_side_effects=True, vmem_limit_bytes=16 << 20
+            collective_id=0, has_side_effects=True, vmem_limit_bytes=24 << 20
         ),
         name="arrive",
-    )(*[pltpu.with_memory_space_constraint(a, pltpu.HBM) for a in (queries[0], out_grad[0], key_states[0], hidden[0], w_value)], index)
-
-    dest_all = index_in[:, 0].reshape(n_x, n_y, rows).transpose(1, 0, 2).reshape(1, slab)
-    ids_all = index_in[:, 1]
-    half = head // 2
-    frequency = rope_base ** (-(np.arange(half, dtype=np.float64) * 2.0 / head))
-    frequency = np.concatenate([frequency, frequency])[None]
-    low = np.arange(rows, dtype=np.float64)[:, None] * frequency
-    consts = [
-        jnp.asarray(np.broadcast_to(frequency, (8, head)), F32),
-        jnp.asarray(np.cos(low), F32),
-        jnp.asarray(np.sin(low), F32),
-    ]
+    )(*kept, index, q_gain[None], k_gain[None], *consts)
+
     tiles = slab // TILE
-    n_docs = 4
     gq, gk, gv, ga = pl.pallas_call(
         functools.partial(attend_kernel, (n_x, n_y, rows, heads, head, n_docs)),
-        out_shape=(wide, narrow, narrow, narrow),
-        in_specs=[VMEM] * 11,
+        out_shape=(sds(stacked, F32), sds((slab, head), F32), narrow, narrow),
+        in_specs=[VMEM] * 5,
         out_specs=(VMEM,) * 4,
         scratch_shapes=[
-            pltpu.VMEM((n_x, heads * rows, head), BF16),
-            pltpu.VMEM((n_x, heads * rows, head), BF16),
-            pltpu.VMEM((slab, head), BF16),
-            pltpu.VMEM((slab, head), BF16),
-            pltpu.VMEM((slab, head), F32),
-            pltpu.VMEM((slab, head), F32),
-            pltpu.VMEM((n_ctx * n_docs, head), F32),
-            pltpu.VMEM((n_ctx * n_docs, head), F32),
+            pltpu.VMEM(stacked, BF16),
             pltpu.VMEM((tiles, TILE, heads * rows), F32),
             pltpu.VMEM((tiles, TILE, heads * rows), F32),
             pltpu.VMEM((slab, head), F32),
-            pltpu.VMEM((slab, head), F32),
-            pltpu.VMEM((heads * rows, head), F32),
+            pltpu.VMEM((head, slab), BF16),
         ],
-        compiler_params=pltpu.CompilerParams(vmem_limit_bytes=44 << 20),
+        compiler_params=pltpu.CompilerParams(vmem_limit_bytes=36 << 20),
         name="attend",
-    )(q_in, g_in, k_in, v_in, dest_all, ids_all, q_gain[None], k_gain[None], *consts)
+    )(qs, g_in, kn, vs, index_in)
 
     out_rows = share // n_ctx
     pad = (out_rows + 15) // 16 * 16
@@ -684,9 +719,11 @@
             sds((rows, model), BF16),
             sds((out_rows, kv_width), F32),
         ),
-        in_specs=[ANY] * 4 + [HBM] * 2 + [ANY],
+        in_specs=[VMEM] * 2 + [ANY] * 2 + [HBM] * 2 + [ANY] + [VMEM] * 6,
         out_specs=(ANY, VMEM, VMEM, VMEM),
         scratch_shapes=[
+            pltpu.VMEM((n_x, rows, width), BF16),
+            pltpu.VMEM((n_y, n_x, rows, head), BF16),
             pltpu.VMEM((3, n_y, n_x, rows, head), BF16),
             pltpu.VMEM((3, n_x, rows, head), BF16),
             pltpu.VMEM((2, n_x, rows, head), BF16),
@@ -705,8 +742,8 @@
             dma((3, n_x)),
             dma((3, n_x)),
             dma((6,)),
-            dma((n_dp, 3, 2)),
-            dma((n_dp, 2)),
+            dma((n_dp, 3, n_x)),
+            dma((n_dp, n_x)),
             dma((n_ctx,)),
             dma((n_ctx,)),
             dma((n_dp,)),
@@ -716,7 +753,7 @@
             collective_id=1, has_side_effects=True, vmem_limit_bytes=32 << 20
         ),
         name="give_back",
-    )(gq, gk, gv, ga, w_value, hidden[0], hf)
+    )(gq, gk, gv, ga, w_value, hidden[0], hf, q_in, k_in, cs, sn, q_gain[None], k_gain[None])
     return (hidden_grad[None], query_grad[None], key_grad[None], weight_grad)
 
 

time: 132 us -> 123 us (0.932); the launches traced: 133 us -> 122 us
  Pallas kernels: 128 us -> 113 us
  local copies, waits for them, and re-layouts: 3.36 us -> 7 us
    pallas_call x1, Pallas kernels: 34 us -> 13.3 us  [on_device(): pl.pallas_call(functools.partial(attend_kernel, (n_x, n_y, rows, heads, h...]
    unnamed x18 -> x22, local copies, waits for them, and re-layouts: 3.34 us -> 7 us
    pallas_call x1, Pallas kernels: 38.4 us -> 41.6 us  [on_device(): pl.pallas_call(functools.partial(arrive_kernel, sizes), out_shape=(wide,...]
    pallas_call x1, Pallas kernels: 55.5 us -> 58.4 us  [on_device(): pl.pallas_call(functools.partial(return_kernel, sizes), out_shape=(sds((r...]
where the time goes in v2:
time: 123 us; the launch traced here: 122 us
  Pallas kernels  113 us (92%)
  local copies, waits for them, and re-layouts  7 us (6%)
    pallas_call x1, Pallas kernels, on_device(): pl.pallas_call(functools.partial(return_kernel, sizes), out_shape=(sds((r...  58.4 us
    pallas_call x1, Pallas kernels, on_device(): pl.pallas_call(functools.partial(arrive_kernel, sizes), out_shape=(wide,...  41.6 us
    pallas_call x1, Pallas kernels, on_device(): pl.pallas_call(functools.partial(attend_kernel, (n_x, n_y, rows, heads, h...  13.3 us
    unnamed x22, local copies, waits for them, and re-layouts  7 us

profile of v2, /device:TPU:25, one launch (start us, length us, event | category | flops | bytes accessed | tf_op | source)
XLA Modules:
  0.0 121.7 jit_solution(17657247551877666277)
XLA Ops:
  0.6 0.7 pad_add_fusion.index
  1.3 0.0 copy-start.2
  1.3 0.8 copy-done.2
  2.2 0.0 copy-start.3
  2.2 0.8 copy-done.3
  3.0 0.0 copy-start.4
  3.0 0.7 copy-done.4
  3.7 0.0 copy-start.5
  3.7 0.7 copy-done.5
  4.3 0.0 copy-start.7
  4.3 0.7 copy-done.7
  5.0 0.0 copy-start
  5.0 41.6 %arrive.1 = (bf16[4,128,1024]{2,1,0:T(8,128)(2,1)S(1)}, bf16[4,128,1024]{2,1,0:T(8,128)(2,1)S(1)}, bf16[4,4,128,128]{3,2,1,0:T(8,128)(2,1)S(1)}, s32[16,2,128]{2...) custom-call(bf16[128,4096]{1,0:T(8,128)(2,1)} %bitcast.18, ...), custom_call_target="tpu_custom_call" | custom-call | tf_op jit(solution)/shard_map/arrive/pallas_call | solution.py:656
  46.6 0.0 copy-start.1
  46.6 0.0 copy-start.6
  46.6 0.0 copy-start.8
  46.6 13.3 %attend.1 = (f32[4,1024,128]{2,1,0:T(8,128)S(1)}, f32[2048,128]{1,0:T(8,128)S(1)}, bf16[4,4,128,128]{3,2,1,0:T(8,128)(2,1)S(1)}, bf16[4,4,128,128]{3,2,1,0:T(8,128)(2,1)S(1)}) custom-call(bf16[4,1024,128]{2,1,0:T(8,128)(2,1)S(1)} %get-tuple-element.22.qs, bf16[4,128,1024]{2,1,0:T(8,128)(2,1)S(1)} %get-tuple-element.23.g_ref, ...), custom_call_target="tpu_custom_call" | custom-call | tf_op jit(solution)/shard_map/attend/pallas_call | solution.py:696
  59.9 0.0 copy-done
  60.0 0.0 copy-done.1
  60.0 0.0 copy-done.6
  60.0 0.0 copy-done.8
  60.0 58.4 %give_back.1 = (bf16[128,4096]{1,0:T(8,128)(2,1)S(1)}, bf16[128,512]{1,0:T(8,128)(2,1)S(1)}, bf16[128,5120]{1,0:T(8,128)(2,1)S(1)}, f32[20,512]{1,0:T(8,128)S(1)}) custom-call(f32[4,1024,128]{2,1,0:T(8,128)S(1)} %get-tuple-element.27.gq_raw, f32[2048,128]{1,0:T(8,128)S(1)} %get-tuple-element.28.gk_raw, bf16[4,4,128,128]{3,2,1,0:T(8,128)(2,1)S(1)} %get-tuple-element.29.gv, ...), custom_call_target="tpu_custom_call" | custom-call | tf_op jit(solution)/shard_map/give_back/pallas_call | solution.py:714
  118.4 1.1 copy.20
  119.5 1.0 copy.21
  120.5 0.7 copy.22
  121.1 0.6 copy.23
Async XLA Ops:
  1.3 0.8 copy-start.2
  2.2 0.8 copy-start.3
  3.0 0.7 copy-start.4
  3.7 0.7 copy-start.5
  4.3 0.7 copy-start.7
  5.0 55.0 %copy-start = (bf16[5120,512]{1,0:T(8,128)(2,1)S(1)}, bf16[5120,512]{1,0:T(8,128)(2,1)}, u32[]{:S(2)}) copy-start(bf16[5120,512]{1,0:T(8,128)(2,1)} %w.3) | copy-start | bytes 15728644
  46.6 13.4 %copy-start.1 = (bf16[1,128,5120]{2,1,0:T(8,128)(2,1)S(1)}, bf16[1,128,5120]{2,1,0:T(8,128)(2,1)}, u32[]{:S(2)}) copy-start(bf16[1,128,5120]{2,1,0:T(8,128)(2,1)} %param.12) | copy-start | bytes 3932164
  46.6 13.4 %copy-start.6 = (f32[128]{0:T(128)S(1)}, f32[128]{0:T(128)}, u32[]{:S(2)}) copy-start(f32[128]{0:T(128)} %param.17) | copy-start | bytes 1540
  46.6 13.4 %copy-start.8 = (f32[128]{0:T(128)S(1)}, f32[128]{0:T(128)}, u32[]{:S(2)}) copy-start(f32[128]{0:T(128)} %param.18) | copy-start | bytes 1540

commit v3 on v2

--- a/solution.py
+++ b/solution.py
@@ -68,9 +68,9 @@
 
 
 def arrive_kernel(
-    sizes, q, g, k, h, w, index, qg_ref, kg_ref, fr_ref, clo_ref, slo_ref,
+    sizes, q, g, k, h, w, index, gain_q, gain_k, table,
     q_o, g_o, k_o, index_o, hf_o, cs, sn, kn, qs, vs,
-    h_v, w_v, v_v, v_o, c0t, s0t, ssem, rsem, ysem, yrem, isem, irem, hssem, hrsem, lsem,
+    h_v, w_v, v_v, v_o, c0t, s0t, qg_ref, kg_ref, tab, ssem, rsem, ysem, yrem, isem, irem, hssem, hrsem, lsem,
 ):
     n_dp, n_x, n_y, rows, width, head, share, win = sizes
     n_ctx, n_z = n_x * n_y, n_dp // 2
@@ -81,6 +81,12 @@
     load_w = pltpu.make_async_copy(w, w_v, lsem.at[1])
     load_h.start()
     load_w.start()
+    small = [
+        pltpu.make_async_copy(a, b, lsem.at[8 + n])
+        for n, (a, b) in enumerate(((gain_q, qg_ref), (gain_k, kg_ref), (table, tab)))
+    ]
+    for copy in small:
+        copy.start()
 
     barrier = pltpu.get_barrier_semaphore()
 
@@ -172,6 +178,8 @@
         idx_copy(d, me, lax.rem(me + n_ctx - d, n_ctx)).wait_recv()
 
     own_idx.wait()
+    for copy in small:
+        copy.wait()
 
     n_docs = c0t.shape[0] // n_ctx
     ids = index_o[:, 1, :]
@@ -184,7 +192,7 @@
     first = jnp.zeros_like(line)
     for d, b in enumerate(bounds):
         first = jnp.where(doc == d + 1, b, first)
-    angle = ((line // n_docs) * rows - first).astype(F32) * fr_ref[:1]
+    angle = ((line // n_docs) * rows - first).astype(F32) * tab[2 * rows : 2 * rows + 1, :]
     c0t[...] = jnp.cos(angle)
     s0t[...] = jnp.sin(angle)
     sign = head_lanes(head)
@@ -201,7 +209,7 @@
         for d, b in enumerate(bounds):
             c0 = jnp.where(row >= b, c0t[pl.ds(i * n_docs + d + 1, 1), :], c0)
             s0 = jnp.where(row >= b, s0t[pl.ds(i * n_docs + d + 1, 1), :], s0)
-        clo, slo = clo_ref[...], slo_ref[...]
+        clo, slo = tab[:rows, :], tab[rows : 2 * rows, :]
         cs[at, :] = clo * c0 - slo * s0
         sn[at, :] = (slo * c0 + clo * s0) * sign
 
@@ -377,6 +385,7 @@
 
     load_w = pltpu.make_async_copy(w, w_v, lsem.at[0])
     load_w.start()
+    dws[...] = jnp.zeros_like(dws)
 
     def hf_pairs(away):
         for d in range(n_z):
@@ -519,28 +528,7 @@
     for ch in range(n_x):
         go(dp, ch, 2, twin)
 
-    reduce_y(1)
-    start_x(1)
-    reduce_y(2)
-    start_x(2)
-    load_w.wait()
-    r2[0, x] = s1[1, x]
-    r2[1, x] = s1[2, x]
-    arrived_x(1)
-    for hd in range(n_x):
-        vg[:, hd * head : (hd + 1) * head] = r2[0, hd]
-
-    model = h_o.shape[1]
-    steps = max(ahead, 1)
-    span = model // steps
-    sub = 256 if span % 256 == 0 else span
-    for t in range(1, steps + 1):
-
-        @pl.loop(0, span // sub)
-        def _(n, t=t):
-            at = pl.ds(pl.multiple_of((t - 1) * span + n * sub, sub), sub)
-            h_o[:, at] = dot(vg[...], w_v[at, :], NT).astype(BF16)
-
+    def relay(t):
         for ch in range(n_x):
             for way, to, hop in ((0, after, n_z - t), (1, before, t)):
                 if takes(t, ch, way):
@@ -549,37 +537,76 @@
                     if takes(t + 1, ch, way):
                         go(slot, ch, way, to)
                     go(slot, ch, 2, twin)
-        if t == 1:
-            arrived_x(2)
-            for hd in range(n_x):
-                gk_o[:, hd * head : (hd + 1) * head] = r2[1, hd]
-        if t == 2 or t == steps:
-            if t == min(2, steps):
-                for i, _, frm in hf_pairs(True):
-                    hf_copy(i, dp, frm).wait_recv()
-                    hft[frm] = hf_v[frm].T
-
-    for t in range(n_z):
-        slot = lax.rem(z + t, n_z) * 2 + 1 - core
+
+    started = [False]
+
+    def weigh(d):
+        slots = [lax.rem(z + d, n_z) * 2 + c for c in (core, 1 - core)]
         for ch in range(n_x):
-            ring(slot, ch, 2, twin).wait_recv()
-
-    group = 4
-    for n in range(n_dp // group):
-        at = slice(n * group, (n + 1) * group)
-        a = jnp.concatenate([hft[e] for e in range(n * group, (n + 1) * group)], axis=1)
-        b = jnp.concatenate([ag[at, hd].reshape(group * rows, head) for hd in range(n_x)], axis=1)
-        if n == 0:
+            ring(slots[1], ch, 2, twin).wait_recv()
+        a = jnp.concatenate([hft[e] for e in slots], axis=1)
+        b = jnp.concatenate(
+            [jnp.concatenate([ag[e, hd] for hd in range(n_x)], axis=1) for e in slots], axis=0
+        )
+        if started[0]:
+            dw[...] += dot(a, b)
+        else:
             dw[...] = dot(a, b)
+            started[0] = True
+
+    model = h_o.shape[1]
+    sub = 256
+
+    def hidden_part(n, parts):
+        span = model // parts
+
+        @pl.loop(0, span // sub)
+        def _(i):
+            at = pl.ds(pl.multiple_of(n * span + i * sub, sub), sub)
+            h_o[:, at] = dot(vg[...], w_v[at, :], NT).astype(BF16)
+
+    def first_half():
+        arrived_x(1)
+        for hd in range(n_x):
+            vg[:, hd * head : (hd + 1) * head] = r2[0, hd]
+        load_w.wait()
+        hidden_part(0, 2)
+
+    reduce_y(1)
+    start_x(1)
+    relay(1)
+    reduce_y(2)
+    start_x(2)
+    r2[0, x] = s1[1, x]
+    r2[1, x] = s1[2, x]
+    for i, _, frm in hf_pairs(True):
+        hf_copy(i, dp, frm).wait_recv()
+        hft[frm] = hf_v[frm].T
+    for t in range(2, ahead):
+        relay(t)
+        if t == 2:
+            weigh(0)
+            first_half()
         else:
-            dw[...] += dot(a, b)
+            for d in (1, 2) if t == 3 else (t - 1,):
+                weigh(d)
+                weigh(n_z - d)
+    if ahead > 1:
+        relay(ahead)
+    for d in range(ahead - 1, n_z - ahead + 2) if ahead > 2 else range(n_z):
+        weigh(d)
+    if ahead < 3:
+        first_half()
+
     off = pl.multiple_of(dp * share - (dp * share) // 128 * 128, 64)
     out_rows = share // n_ctx
-    pad = dws.shape[1]
-    for c in range(n_ctx):
-        dws[c, :out_rows, :] = dw[pl.ds(off, share), :][c * out_rows : (c + 1) * out_rows].astype(BF16)
-        if pad > out_rows:
-            dws[c, out_rows:, :] = jnp.zeros((pad - out_rows, n_x * head), BF16)
+    for o in range(0, win - share + 1, 64):
+
+        @pl.when(off == o)
+        def _(o=o):
+            for c in range(n_ctx):
+                at = slice(o + c * out_rows, o + (c + 1) * out_rows)
+                dws[c, :out_rows, :] = dw[at, :].astype(BF16)
 
     def w_copy(d, to, frm):
         return send(dws.at[to], dwr.at[frm], ws.at[d], wr.at[d], dp, to)
@@ -589,6 +616,10 @@
         w_copy(d, lax.rem(me + d, n_ctx), me).start()
 
     dwr[me] = dws[me]
+    hidden_part(1, 2)
+    arrived_x(2)
+    for hd in range(n_x):
+        gk_o[:, hd * head : (hd + 1) * head] = r2[1, hd]
     for n in range(2):
         q_copy(n, 0, x, x).wait()
         for d in range(1, n_x):
@@ -641,17 +672,18 @@
     frequency = rope_base ** (-(np.arange(half, dtype=np.float64) * 2.0 / head))
     frequency = np.concatenate([frequency, frequency])[None]
     low = np.arange(rows, dtype=np.float64)[:, None] * frequency
-    consts = [
-        jnp.asarray(np.broadcast_to(frequency, (8, head)), F32),
-        jnp.asarray(np.cos(low), F32),
-        jnp.asarray(np.sin(low), F32),
-    ]
+    table = np.concatenate([np.cos(low), np.sin(low), np.repeat(frequency, 8, axis=0)])
+    table = jnp.asarray(table, F32)
     n_docs = 4
     stacked = (n_x, heads * rows, head)
     flat = sds((slab, head), BF16)
     kept = [
         pltpu.with_memory_space_constraint(a, pltpu.HBM)
         for a in (queries[0], out_grad[0], key_states[0], hidden[0], w_value)
+    ]
+    tail = [
+        pltpu.with_memory_space_constraint(a, pltpu.HBM)
+        for a in (q_gain[None], k_gain[None], table)
     ]
     q_in, g_in, k_in, index_in, hf, cs, sn, kn, qs, vs = pl.pallas_call(
         functools.partial(arrive_kernel, sizes),
@@ -667,7 +699,7 @@
             sds(stacked, BF16),
             flat,
         ),
-        in_specs=[HBM] * 5 + [ANY] + [VMEM] * 5,
+        in_specs=[HBM] * 5 + [ANY] + [HBM] * 3,
         out_specs=(VMEM, ANY, VMEM, VMEM, ANY) + (VMEM,) * 5,
         scratch_shapes=[
             pltpu.VMEM((rows, model), BF16),
@@ -676,6 +708,9 @@
             pltpu.VMEM((n_y, n_x, rows, head), BF16),
             pltpu.VMEM((n_ctx * n_docs, head), F32),
             pltpu.VMEM((n_ctx * n_docs, head), F32),
+            pltpu.VMEM((1, head), F32),
+            pltpu.VMEM((1, head), F32),
+            pltpu.VMEM((2 * rows + 8, head), F32),
             dma((4, n_x)),
             dma((4, n_x)),
             dma((2, n_y)),
@@ -684,13 +719,13 @@
             dma((n_ctx,)),
             dma((n_dp,)),
             dma((n_dp,)),
-            dma((8,)),
+            dma((11,)),
         ],
         compiler_params=pltpu.CompilerParams(
             collective_id=0, has_side_effects=True, vmem_limit_bytes=24 << 20
         ),
         name="arrive",
-    )(*kept, index, q_gain[None], k_gain[None], *consts)
+    )(*kept, index, *tail)
 
     tiles = slab // TILE
     gq, gk, gv, ga = pl.pallas_call(
@@ -711,14 +746,15 @@
 
     out_rows = share // n_ctx
     pad = (out_rows + 15) // 16 * 16
+    results = (
+        sds((rows, n_x * width), BF16),
+        sds((rows, kv_width), BF16),
+        sds((rows, model), BF16),
+        sds((out_rows, kv_width), F32),
+    )
     query_grad, key_grad, hidden_grad, weight_grad = pl.pallas_call(
         functools.partial(return_kernel, sizes),
-        out_shape=(
-            sds((rows, n_x * width), BF16),
-            sds((rows, kv_width), BF16),
-            sds((rows, model), BF16),
-            sds((out_rows, kv_width), F32),
-        ),
+        out_shape=results,
         in_specs=[VMEM] * 2 + [ANY] * 2 + [HBM] * 2 + [ANY] + [VMEM] * 6,
         out_specs=(ANY, VMEM, VMEM, VMEM),
         scratch_shapes=[

time: 123 us -> 115 us (0.935)
  Pallas kernels: 113 us -> 109 us
  local copies, waits for them, and re-layouts: 7 us -> 3.33 us
    pallas_call x1, Pallas kernels: 58.4 us -> 50.6 us  [on_device(): pl.pallas_call(functools.partial(return_kernel, sizes), out_shape=results...]
    unnamed x22 -> x12, local copies, waits for them, and re-layouts: 7 us -> 3.33 us
    pallas_call x1, Pallas kernels: 13.3 us -> 16.6 us  [on_device(): pl.pallas_call(functools.partial(attend_kernel, (n_x, n_y, rows, heads, h...]
where the time goes in v3:
time: 115 us; the launch traced here: 114 us
  Pallas kernels  109 us (95%)
  local copies, waits for them, and re-layouts  3.33 us (3%)
    pallas_call x1, Pallas kernels, on_device(): pl.pallas_call(functools.partial(return_kernel, sizes), out_shape=results...  50.6 us
    pallas_call x1, Pallas kernels, on_device(): pl.pallas_call(functools.partial(arrive_kernel, sizes), out_shape=(wide,...  41.9 us
    pallas_call x1, Pallas kernels, on_device(): pl.pallas_call(functools.partial(attend_kernel, (n_x, n_y, rows, heads, h...  16.6 us
    unnamed x12, local copies, waits for them, and re-layouts  3.33 us

profile of v3, /device:TPU:25, one launch (start us, length us, event | category | flops | bytes accessed | tf_op | source)
XLA Modules:
  0.0 113.8 jit_solution(4148878102300208676)
XLA Ops:
  0.6 0.7 pad_add_fusion.index
  1.3 0.0 copy-start
  1.3 41.9 %arrive.1 = (bf16[4,128,1024]{2,1,0:T(8,128)(2,1)S(1)}, bf16[4,128,1024]{2,1,0:T(8,128)(2,1)S(1)}, bf16[4,4,128,128]{3,2,1,0:T(8,128)(2,1)S(1)}, s32[16,2,128]{2...) custom-call(bf16[128,4096]{1,0:T(8,128)(2,1)} %bitcast.18, ...), custom_call_target="tpu_custom_call" | custom-call | tf_op jit(solution)/shard_map/arrive/pallas_call | solution.py:688
  43.2 0.0 copy-start.1
  43.2 0.0 copy-start.2
  43.3 0.0 copy-start.3
  43.3 16.6 %attend.1 = (f32[4,1024,128]{2,1,0:T(8,128)S(1)}, f32[2048,128]{1,0:T(8,128)S(1)}, bf16[4,4,128,128]{3,2,1,0:T(8,128)(2,1)S(1)}, bf16[4,4,128,128]{3,2,1,0:T(8,128)(2,1)S(1)}) custom-call(bf16[4,1024,128]{2,1,0:T(8,128)(2,1)S(1)} %get-tuple-element.22.qs, bf16[4,128,1024]{2,1,0:T(8,128)(2,1)S(1)} %get-tuple-element.23.g_ref, ...), custom_call_target="tpu_custom_call" | custom-call | tf_op jit(solution)/shard_map/attend/pallas_call | solution.py:731
  59.8 0.0 copy-done
  59.8 0.0 copy-done.1
  59.8 0.0 copy-done.2
  59.9 0.0 copy-done.3
  59.9 50.6 %give_back.1 = (bf16[128,4096]{1,0:T(8,128)(2,1)S(1)}, bf16[128,512]{1,0:T(8,128)(2,1)S(1)}, bf16[128,5120]{1,0:T(8,128)(2,1)S(1)}, f32[20,512]{1,0:T(8,128)S(1)}) custom-call(f32[4,1024,128]{2,1,0:T(8,128)S(1)} %get-tuple-element.27.gq_raw, f32[2048,128]{1,0:T(8,128)S(1)} %get-tuple-element.28.gk_raw, bf16[4,4,128,128]{3,2,1,0:T(8,128)(2,1)S(1)} %get-tuple-element.29.gv, ...), custom_call_target="tpu_custom_call" | custom-call | tf_op jit(solution)/shard_map/give_back/pallas_call | solution.py:755
  110.5 1.1 copy.18
  111.5 1.0 copy.19
  112.5 0.7 copy.20
  113.2 0.6 copy.21
Async XLA Ops:
  1.3 58.5 %copy-start = (bf16[5120,512]{1,0:T(8,128)(2,1)S(1)}, bf16[5120,512]{1,0:T(8,128)(2,1)}, u32[]{:S(2)}) copy-start(bf16[5120,512]{1,0:T(8,128)(2,1)} %w.3) | copy-start | bytes 15728644
  43.2 16.6 %copy-start.1 = (bf16[1,128,5120]{2,1,0:T(8,128)(2,1)S(1)}, bf16[1,128,5120]{2,1,0:T(8,128)(2,1)}, u32[]{:S(2)}) copy-start(bf16[1,128,5120]{2,1,0:T(8,128)(2,1)} %param.10) | copy-start | bytes 3932164
  43.2 16.6 %copy-start.2 = (f32[128]{0:T(128)S(1)}, f32[128]{0:T(128)}, u32[]{:S(2)}) copy-start(f32[128]{0:T(128)} %param.15) | copy-start | bytes 1540
  43.3 16.6 %copy-start.3 = (f32[128]{0:T(128)S(1)}, f32[128]{0:T(128)}, u32[]{:S(2)}) copy-start(f32[128]{0:T(128)} %param.16) | copy-start | bytes 1540

commit v4 on v3

--- a/solution.py
+++ b/solution.py
@@ -486,6 +486,12 @@
     start_q(0)
     start_y(1)
 
+    for copy in hf_loads:
+        copy.wait()
+    for i, _, frm in hf_pairs(False):
+        hft[frm] = hf_v[frm].T
+    reduce_y(0)
+    start_x(0)
     @pl.loop(0, n_ctx)
     def _(i):
         at = pl.ds(pl.multiple_of(i * rows, rows), rows)
@@ -493,15 +499,9 @@
         u = k_in[i % n_y, i // n_y].astype(F32)
         gk[i % n_y, i // n_y] = normrope_back(u, gz, kg_ref[...], cs[at, :], sn[at, :]).astype(BF16)
 
-    reduce_y(0)
-    start_x(0)
     start_y(2)
     start_q(1)
     ag[dp, x] = s1[0, x]
-    for copy in hf_loads:
-        copy.wait()
-    for i, _, frm in hf_pairs(False):
-        hft[frm] = hf_v[frm].T
     arrived_x(0)
 
     def piece(slot, ch):

time: 115 us -> 115 us (level)
    pallas_call x1, Pallas kernels: 16.6 us -> 11.1 us  [on_device(): pl.pallas_call(functools.partial(attend_kernel, (n_x, n_y, rows, heads, h...]
    pallas_call x1, Pallas kernels: 50.6 us -> 55.8 us  [on_device(): pl.pallas_call(functools.partial(return_kernel, sizes), out_shape=results...]
where the time goes in v4:
time: 115 us; the launch traced here: 114 us
  Pallas kernels  109 us (95%)
  local copies, waits for them, and re-layouts  3.33 us (3%)
    pallas_call x1, Pallas kernels, on_device(): pl.pallas_call(functools.partial(return_kernel, sizes), out_shape=results...  55.8 us
    pallas_call x1, Pallas kernels, on_device(): pl.pallas_call(functools.partial(arrive_kernel, sizes), out_shape=(wide,...  41.9 us
    pallas_call x1, Pallas kernels, on_device(): pl.pallas_call(functools.partial(attend_kernel, (n_x, n_y, rows, heads, h...  11.1 us
    unnamed x12, local copies, waits for them, and re-layouts  3.33 us

profile of v4, /device:TPU:25, one launch (start us, length us, event | category | flops | bytes accessed | tf_op | source)
XLA Modules:
  0.0 113.6 jit_solution(5886280944150262909)
XLA Ops:
  0.6 0.7 pad_add_fusion.index
  1.3 0.0 copy-start
  1.3 41.9 %arrive.1 = (bf16[4,128,1024]{2,1,0:T(8,128)(2,1)S(1)}, bf16[4,128,1024]{2,1,0:T(8,128)(2,1)S(1)}, bf16[4,4,128,128]{3,2,1,0:T(8,128)(2,1)S(1)}, s32[16,2,128]{2...) custom-call(bf16[128,4096]{1,0:T(8,128)(2,1)} %bitcast.18, ...), custom_call_target="tpu_custom_call" | custom-call | tf_op jit(solution)/shard_map/arrive/pallas_call | solution.py:688
  43.2 0.0 copy-start.1
  43.2 0.0 copy-start.2
  43.3 0.0 copy-start.3
  43.3 11.1 %attend.1 = (f32[4,1024,128]{2,1,0:T(8,128)S(1)}, f32[2048,128]{1,0:T(8,128)S(1)}, bf16[4,4,128,128]{3,2,1,0:T(8,128)(2,1)S(1)}, bf16[4,4,128,128]{3,2,1,0:T(8,128)(2,1)S(1)}) custom-call(bf16[4,1024,128]{2,1,0:T(8,128)(2,1)S(1)} %get-tuple-element.22.qs, bf16[4,128,1024]{2,1,0:T(8,128)(2,1)S(1)} %get-tuple-element.23.g_ref, ...), custom_call_target="tpu_custom_call" | custom-call | tf_op jit(solution)/shard_map/attend/pallas_call | solution.py:731
  54.4 0.0 copy-done
  54.4 0.0 copy-done.1
  54.4 0.0 copy-done.2
  54.4 0.0 copy-done.3
  54.5 55.8 %give_back.1 = (bf16[128,4096]{1,0:T(8,128)(2,1)S(1)}, bf16[128,512]{1,0:T(8,128)(2,1)S(1)}, bf16[128,5120]{1,0:T(8,128)(2,1)S(1)}, f32[20,512]{1,0:T(8,128)S(1)}) custom-call(f32[4,1024,128]{2,1,0:T(8,128)S(1)} %get-tuple-element.27.gq_raw, f32[2048,128]{1,0:T(8,128)S(1)} %get-tuple-element.28.gk_raw, bf16[4,4,128,128]{3,2,1,0:T(8,128)(2,1)S(1)} %get-tuple-element.29.gv, ...), custom_call_target="tpu_custom_call" | custom-call | tf_op jit(solution)/shard_map/give_back/pallas_call | solution.py:755
  110.3 1.1 copy.18
  111.3 1.0 copy.19
  112.3 0.7 copy.20
  112.9 0.6 copy.21
Async XLA Ops:
  1.3 53.1 %copy-start = (bf16[5120,512]{1,0:T(8,128)(2,1)S(1)}, bf16[5120,512]{1,0:T(8,128)(2,1)}, u32[]{:S(2)}) copy-start(bf16[5120,512]{1,0:T(8,128)(2,1)} %w.3) | copy-start | bytes 15728644
  43.2 11.2 %copy-start.1 = (bf16[1,128,5120]{2,1,0:T(8,128)(2,1)S(1)}, bf16[1,128,5120]{2,1,0:T(8,128)(2,1)}, u32[]{:S(2)}) copy-start(bf16[1,128,5120]{2,1,0:T(8,128)(2,1)} %param.10) | copy-start | bytes 3932164
  43.2 11.2 %copy-start.2 = (f32[128]{0:T(128)S(1)}, f32[128]{0:T(128)}, u32[]{:S(2)}) copy-start(f32[128]{0:T(128)} %param.15) | copy-start | bytes 1540
  43.3 11.2 %copy-start.3 = (f32[128]{0:T(128)S(1)}, f32[128]{0:T(128)}, u32[]{:S(2)}) copy-start(f32[128]{0:T(128)} %param.16) | copy-start | bytes 1540
